TPU v7x, 32 devices: a whole 2x2x4 slice. The times are simulated.
32 devices in a mesh: dp: 2 (over x), tp: 4 (over z), cp: 4 (over y, core).
Axes of the slice: x: 2, y: 2, z: 4, core: 2. Of those that a mesh axis runs over, the one named last changes fastest.
Arguments:
- c_latent: bfloat16 [4096, 512], P(('dp', 'cp')), parts along dimension 0
- k_rope: bfloat16 [4096, 64], P(('dp', 'cp')), parts along dimension 0
- q_heads: bfloat16 [4096, 128, 192], P(('dp', 'cp'), 'tp'), parts along dimension 0
- d_out: bfloat16 [4096, 128, 128], P(('dp', 'cp'), 'tp'), parts along dimension 0
- w_uk: bfloat16 [512, 128, 128], P(None, 'tp')
- w_uv: bfloat16 [512, 128, 128], P(None, 'tp')
Outputs:
- output 1: bfloat16 [4096, 128, 128], P(('dp', 'cp'), 'tp'), parts along dimension 0
- output 2: float32 [4096, 128, 192], P(('dp', 'cp'), 'tp'), parts along dimension 0
- output 3: float32 [4096, 512], P(('dp', 'cp')), parts along dimension 0
- output 4: float32 [4096, 64], P(('dp', 'cp')), parts along dimension 0
- output 5: float32 [1024, 128, 128], P('dp', 'tp'), parts along dimension 0
- output 6: float32 [1024, 128, 128], P('dp', 'tp'), parts along dimension 0
There are 2 independent parts. A program takes and returns all parts, laid end to end along the dimension named above; an argument that names none is the same for every part.
All inputs are finite; a program needn't handle non-finite values.
Results may differ from a plain program's by a relative error of at most 0.0148993.
Values are sent between devices in bfloat16 or wider.
A program may use at most 1 GiB of HBM per device.

v0:
```python
import jax
import jax.numpy as jnp
from jax import lax
from jax.sharding import PartitionSpec as P

NEG_BIG = -1.0e30


def project_block(c_blk, w_uk, w_uv):
    knope_blk = jnp.einsum('kr,rhd->khd', c_blk, w_uk, preferred_element_type=jnp.float32)
    v_blk = jnp.einsum('kr,rhd->khd', c_blk, w_uv, preferred_element_type=jnp.float32)
    return knope_blk.astype(jnp.bfloat16), v_blk.astype(jnp.bfloat16)


def block_scores(q_nope, q_rope, knope_blk, rope_blk, qk_scale, key_mask):
    scores = jnp.einsum('qhd,khd->qhk', q_nope, knope_blk, preferred_element_type=jnp.float32)
    scores = scores + jnp.einsum('qhd,kd->qhk', q_rope, rope_blk, preferred_element_type=jnp.float32)
    scores = scores * qk_scale
    if key_mask is None:
        return scores
    return jnp.where(key_mask[:, None, :], scores, NEG_BIG)


def forward_update(soft_state, q_nope, q_rope, c_blk, rope_blk, w_uk, w_uv, qk_scale, key_mask):
    run_max, run_sum, out_acc = soft_state
    knope_blk, v_blk = project_block(c_blk, w_uk, w_uv)
    scores = block_scores(q_nope, q_rope, knope_blk, rope_blk, qk_scale, key_mask)
    new_max = jnp.maximum(run_max, jnp.max(scores, axis=-1))
    rescale = jnp.exp(run_max - new_max)
    prob_blk = jnp.exp(scores - new_max[..., None])
    new_sum = run_sum * rescale + jnp.sum(prob_blk, axis=-1)
    pv_part = jnp.einsum('qhk,khd->qhd', prob_blk.astype(jnp.bfloat16), v_blk, preferred_element_type=jnp.float32)
    return (new_max, new_sum, out_acc * rescale[..., None] + pv_part)


def backward_block(q_nope, q_rope, d_out, log_norm, d_dot, c_blk, rope_blk, w_uk, w_uv, qk_scale, key_mask):
    knope_blk, v_blk = project_block(c_blk, w_uk, w_uv)
    scores = block_scores(q_nope, q_rope, knope_blk, rope_blk, qk_scale, key_mask)
    prob_blk = jnp.exp(scores - log_norm[..., None])
    d_prob = jnp.einsum('qhd,khd->qhk', d_out, v_blk, preferred_element_type=jnp.float32)
    d_score = (prob_blk * (d_prob - d_dot[..., None]) * qk_scale).astype(jnp.bfloat16)
    dq_nope = jnp.einsum('qhk,khd->qhd', d_score, knope_blk, preferred_element_type=jnp.float32)
    dq_rope = jnp.einsum('qhk,kd->qhd', d_score, rope_blk, preferred_element_type=jnp.float32)
    dk_nope = jnp.einsum('qhk,qhd->khd', d_score, q_nope, preferred_element_type=jnp.float32).astype(jnp.bfloat16)
    dk_rope = jnp.einsum('qhk,qhd->kd', d_score, q_rope, preferred_element_type=jnp.float32)
    dv_blk = jnp.einsum('qhk,qhd->khd', prob_blk.astype(jnp.bfloat16), d_out, preferred_element_type=jnp.float32).astype(jnp.bfloat16)
    dc_blk = jnp.einsum('khd,rhd->kr', dk_nope, w_uk, preferred_element_type=jnp.float32) + jnp.einsum('khd,rhd->kr', dv_blk, w_uv, preferred_element_type=jnp.float32)
    dw_k = jnp.einsum('kr,khd->rhd', c_blk, dk_nope, preferred_element_type=jnp.float32)
    dw_v = jnp.einsum('kr,khd->rhd', c_blk, dv_blk, preferred_element_type=jnp.float32)
    return (dq_nope, dq_rope, dc_blk, dk_rope, dw_k, dw_v)


def add_lower(full_arr, part_arr):
    split_at = part_arr.shape[0]
    return jnp.concatenate([full_arr[:split_at] + part_arr, full_arr[split_at:]], axis=0)


def add_upper(full_arr, part_arr):
    split_at = full_arr.shape[0] - part_arr.shape[0]
    return jnp.concatenate([full_arr[:split_at], full_arr[split_at:] + part_arr], axis=0)


def solution(mesh):
    n_cp = mesh.shape['cp']
    shift_perm = [(src_dev, (src_dev + 1) % n_cp) for src_dev in range(n_cp)]
    seq_spec = P(('dp', 'cp'), None)
    head_spec = P(('dp', 'cp'), 'tp', None)
    weight_spec = P(None, 'tp', None)
    grad_spec = P('dp', 'tp', None)

    def device_fn(c_latent, k_rope, q_heads, d_out, w_uk, w_uv):
        tok_rows = c_latent.shape[0]
        half_len = tok_rows // 2
        n_heads = q_heads.shape[1]
        d_nope = w_uk.shape[2]
        d_val = w_uv.shape[2]
        qk_scale = q_heads.shape[2] ** -0.5
        my_idx = lax.axis_index('cp')
        q_nope = q_heads[:, :, :d_nope]
        q_rope = q_heads[:, :, d_nope:]
        half_offsets = jnp.arange(half_len)
        positions = jnp.concatenate([my_idx * half_len + half_offsets, (2 * n_cp - 1 - my_idx) * half_len + half_offsets])
        diag_mask = positions[None, :] <= positions[:, None]

        soft_state = (jnp.full((tok_rows, n_heads), NEG_BIG, jnp.float32), jnp.zeros((tok_rows, n_heads), jnp.float32), jnp.zeros((tok_rows, n_heads, d_val), jnp.float32))
        soft_state = forward_update(soft_state, q_nope, q_rope, c_latent, k_rope, w_uk, w_uv, qk_scale, diag_mask)

        def forward_hop(hop_idx, loop_carry):
            c_blk, rope_blk, state_in = loop_carry
            c_blk = lax.ppermute(c_blk, 'cp', shift_perm)
            rope_blk = lax.ppermute(rope_blk, 'cp', shift_perm)
            src_idx = (my_idx - hop_idx) % n_cp

            def earlier_keys(state_cur):
                return forward_update(state_cur, q_nope, q_rope, c_blk[:half_len], rope_blk[:half_len], w_uk, w_uv, qk_scale, None)

            def later_queries(state_cur):
                upper_state = forward_update(tuple(part_arr[half_len:] for part_arr in state_cur), q_nope[half_len:], q_rope[half_len:], c_blk, rope_blk, w_uk, w_uv, qk_scale, None)
                return tuple(jnp.concatenate([old_arr[:half_len], new_arr], axis=0) for old_arr, new_arr in zip(state_cur, upper_state))

            return (c_blk, rope_blk, lax.cond(src_idx < my_idx, earlier_keys, later_queries, state_in))

        soft_state = lax.fori_loop(1, n_cp, forward_hop, (c_latent, k_rope, soft_state))[2]
        run_max, run_sum, out_acc = soft_state
        out_wide = out_acc / run_sum[..., None]
        log_norm = run_max + jnp.log(run_sum)
        d_dot = jnp.sum(d_out.astype(jnp.float32) * out_wide, axis=-1)
        grad_acc = backward_block(q_nope, q_rope, d_out, log_norm, d_dot, c_latent, k_rope, w_uk, w_uv, qk_scale, diag_mask)

        def backward_hop(hop_idx, loop_carry):
            c_blk, rope_blk, acc_in = loop_carry
            c_blk = lax.ppermute(c_blk, 'cp', shift_perm)
            rope_blk = lax.ppermute(rope_blk, 'cp', shift_perm)
            dc_acc = lax.ppermute(acc_in[2], 'cp', shift_perm)
            drope_acc = lax.ppermute(acc_in[3], 'cp', shift_perm)
            src_idx = (my_idx - hop_idx) % n_cp

            def earlier_keys(acc_cur):
                blk_grads = backward_block(q_nope, q_rope, d_out, log_norm, d_dot, c_blk[:half_len], rope_blk[:half_len], w_uk, w_uv, qk_scale, None)
                return (acc_cur[0] + blk_grads[0], acc_cur[1] + blk_grads[1], add_lower(acc_cur[2], blk_grads[2]), add_lower(acc_cur[3], blk_grads[3]), acc_cur[4] + blk_grads[4], acc_cur[5] + blk_grads[5])

            def later_queries(acc_cur):
                blk_grads = backward_block(q_nope[half_len:], q_rope[half_len:], d_out[half_len:], log_norm[half_len:], d_dot[half_len:], c_blk, rope_blk, w_uk, w_uv, qk_scale, None)
                return (add_upper(acc_cur[0], blk_grads[0]), add_upper(acc_cur[1], blk_grads[1]), acc_cur[2] + blk_grads[2], acc_cur[3] + blk_grads[3], acc_cur[4] + blk_grads[4], acc_cur[5] + blk_grads[5])

            acc_mid = (acc_in[0], acc_in[1], dc_acc, drope_acc, acc_in[4], acc_in[5])
            return (c_blk, rope_blk, lax.cond(src_idx < my_idx, earlier_keys, later_queries, acc_mid))

        grad_acc = lax.fori_loop(1, n_cp, backward_hop, (c_latent, k_rope, grad_acc))[2]
        dq_nope, dq_rope, dc_acc, drope_acc, dw_k, dw_v = grad_acc
        dc_acc = lax.ppermute(dc_acc, 'cp', shift_perm)
        drope_acc = lax.ppermute(drope_acc, 'cp', shift_perm)
        return (out_wide.astype(jnp.bfloat16),
                jnp.concatenate([dq_nope, dq_rope], axis=-1),
                lax.psum(dc_acc, 'tp'),
                lax.psum(drope_acc, 'tp'),
                lax.psum(dw_k, 'cp'),
                lax.psum(dw_v, 'cp'))

    return jax.shard_map(device_fn, mesh=mesh,
                         in_specs=(seq_spec, seq_spec, head_spec, head_spec, weight_spec, weight_spec),
                         out_specs=(head_spec, head_spec, seq_spec, seq_spec, grad_spec, grad_spec),
                         check_vma=False)
```

profile of v0, /device:TPU:0, one launch (start us, length us, event | category | flops | bytes accessed | tf_op | source)
XLA Modules:
  0.0 1341.5 jit_solution(13639925285045451168)
XLA Ops:
  24.5 16.8 %fusion.225 = f32[32,512,512]{2,1,0:T(8,128)} fusion(bf16[512,32,128]{2,0,1:T(8,128)(2,1)S(1)} %convolution_convert_fusion.6, bf16[512,32,192]{0,2,1:T(8,128)(2,1)} %param.16), kind=kOutput, calls=%fused_computation.206 | convolution fusion | flops 2147483648 | bytes 41943040 | tf_op jit(solution)/shard_map/qhd,khd->qhk/dot_general | solution.py:16
  42.1 26.2 %fusion.229 = (f32[512,32]{0,1:T(8,128)S(1)}, f32[512,32,512]{0,2,1:T(8,128)}) fusion(bf16[512,64]{0,1:T(8,128)(2,1)} %copy.230, bf16[512,32,192]{0,2,1:T(8,128)(2,1)} %param.16, f32[32,512,512]{2,1,0:T(8,128)} %fusion.225, pred[512,512]{0,1:T(8,128)(4,1)S(1)} %broadcast_compare_fusion), kind=kOutput, calls=%fused_computation.210 | convolution fusion | flops 1107279872 | bytes 69599232 | tf_op jit(solution)/shard_map/qhd,kd->qhk/dot_general | solution.py:17
  68.4 13.3 fusion.171
  93.7 17.9 %bitcast_add_fusion.13 = f32[512,32,128]{0,2,1:T(8,128)} fusion(f32[512,32]{0,1:T(8,128)S(1)} %get-tuple-element.990, bf16[512,32,128]{2,0,1:T(8,128)(2,1)} %convolution_convert_fusion.5, f32[512,32,512]{0,2,1:T(8,128)} %get-tuple-element.993, f32[512,32]{0,1:T(8,128)S(1)} %broadcast_maximum_fusion), kind=kOutput, calls=%fused_computation.159 | convolution fusion | flops 2166358016 | bytes 46268416 | tf_op jit(solution)/shard_map/qhk,khd->qhd/dot_general | solution.py:32
  111.6 233.6 %while.52 = (s32[]{:T(128)}, bf16[512,512]{1,0:T(8,128)(2,1)S(1)}, bf16[512,64]{0,1:T(8,128)(2,1)S(1)}, f32[512,32]{0,1:T(8,128)S(1)}, f32[512,32]{0,1:T(8,128)S...) while((s32[]{:T(128)}, bf16[512,512]{1,0:T(8,128)(2,1)S(1)}, ...), condition=%wide.region_9.10_spmd, body=%wide.region_2.9_spmd.sunk | while | flops 7017119744 | bytes 151388720 | solution.py:103
  141.4 58.2 %conditional.4 = (f32[512,32]{0,1:T(8,128)}, f32[512,32]{0,1:T(8,128)S(1)}, f32[512,32,128]{0,2,1:T(8,128)}) conditional(s32[]{:T(128)} %convert_element_type.187, (f32[512,32]{0,1:T(8,128)S(1)}, bf16[512,512]{1,0:T(8,128)(2,1)S(1)}, bf16[512,32,128]{2,1,0:T(8,128)(2,1)}, bf16[512,32,128]{2,0,1:T(8,128)(2,1)}, bf16[512,32,64]{0,2,1:T(8,128)(2,1)}, ...), branch_computations={%region_3.5_spmd, %region_6.8_spmd} | conditional | flops 7017119744 | bytes 147718208 | solution.py:101
  141.4 13.2 fusion.11
  154.7 10.9 fusion.227
  174.4 16.6 %bitcast_add_fusion.1 = f32[256,32,128]{0,2,1:T(8,128)} fusion(f32[512,32,128]{0,2,1:T(8,128)} %get-tuple-element.778, f32[256,32]{0,1:T(8,128)S(1)} %get-tuple-element.977, f32[256,32,512]{0,2,1:T(8,128)} %get-tuple-element.983, f32[256,32]{0,1:T(8,128)S(1)} %slice_maximum_fusion, bf16[512,32,128]{2,1,0:T(8,128)(2,1)} %get-tuple-element.779, ...), kind=kOutput, calls=%fused_computation.8 | convolution fusion | flops 3233808384 | bytes 29949952 | tf_op jit(solution)/shard_map/while/body/eval_jaxpr/cond/branch_0_fun/qhk,khd->qhd/dot_general | solution.py:32
  209.9 58.3 %conditional.4 = (f32[512,32]{0,1:T(8,128)}, f32[512,32]{0,1:T(8,128)S(1)}, f32[512,32,128]{0,2,1:T(8,128)}) conditional(s32[]{:T(128)} %convert_element_type.187, (f32[512,32]{0,1:T(8,128)S(1)}, bf16[512,512]{1,0:T(8,128)(2,1)S(1)}, bf16[512,32,128]{2,1,0:T(8,128)(2,1)}, bf16[512,32,128]{2,0,1:T(8,128)(2,1)}, bf16[512,32,64]{0,2,1:T(8,128)(2,1)}, ...), branch_computations={%region_3.5_spmd, %region_6.8_spmd} | conditional | flops 7017119744 | bytes 147718208 | solution.py:101
  209.9 13.2 fusion.11
  223.2 11.0 fusion.227
  242.9 16.6 %bitcast_add_fusion.1 = f32[256,32,128]{0,2,1:T(8,128)} fusion(f32[512,32,128]{0,2,1:T(8,128)} %get-tuple-element.778, f32[256,32]{0,1:T(8,128)S(1)} %get-tuple-element.977, f32[256,32,512]{0,2,1:T(8,128)} %get-tuple-element.983, f32[256,32]{0,1:T(8,128)S(1)} %slice_maximum_fusion, bf16[512,32,128]{2,1,0:T(8,128)(2,1)} %get-tuple-element.779, ...), kind=kOutput, calls=%fused_computation.8 | convolution fusion | flops 3233808384 | bytes 29949952 | tf_op jit(solution)/shard_map/while/body/eval_jaxpr/cond/branch_0_fun/qhk,khd->qhd/dot_general | solution.py:32
  278.4 58.3 %conditional.4 = (f32[512,32]{0,1:T(8,128)}, f32[512,32]{0,1:T(8,128)S(1)}, f32[512,32,128]{0,2,1:T(8,128)}) conditional(s32[]{:T(128)} %convert_element_type.187, (f32[512,32]{0,1:T(8,128)S(1)}, bf16[512,512]{1,0:T(8,128)(2,1)S(1)}, bf16[512,32,128]{2,1,0:T(8,128)(2,1)}, bf16[512,32,128]{2,0,1:T(8,128)(2,1)}, bf16[512,32,64]{0,2,1:T(8,128)(2,1)}, ...), branch_computations={%region_3.5_spmd, %region_6.8_spmd} | conditional | flops 7017119744 | bytes 147718208 | solution.py:101
  278.4 13.2 fusion.11
  291.7 11.0 fusion.227
  311.4 16.6 %bitcast_add_fusion.1 = f32[256,32,128]{0,2,1:T(8,128)} fusion(f32[512,32,128]{0,2,1:T(8,128)} %get-tuple-element.778, f32[256,32]{0,1:T(8,128)S(1)} %get-tuple-element.977, f32[256,32,512]{0,2,1:T(8,128)} %get-tuple-element.983, f32[256,32]{0,1:T(8,128)S(1)} %slice_maximum_fusion, bf16[512,32,128]{2,1,0:T(8,128)(2,1)} %get-tuple-element.779, ...), kind=kOutput, calls=%fused_computation.8 | convolution fusion | flops 3233808384 | bytes 29949952 | tf_op jit(solution)/shard_map/while/body/eval_jaxpr/cond/branch_0_fun/qhk,khd->qhd/dot_general | solution.py:32
  346.0 10.2 copy.74
  356.2 20.1 %fusion.196 = bf16[32,512,128]{2,1,0:T(8,128)(2,1)} fusion(f32[512,32,512]{0,2,1:T(8,128)} %get-tuple-element.993, f32[512,32]{0,1:T(8,128)} %log_add_fusion, bf16[512,32,128]{2,1,0:T(8,128)(2,1)} %param.17), kind=kOutput, calls=%fused_computation.174 | convolution fusion | flops 2166358016 | bytes 42008576 | tf_op jit(solution)/shard_map/qhk,qhd->khd/dot_general | solution.py:46
  386.0 22.1 %fusion.167 = bf16[512,32,512]{0,2,1:T(8,128)(2,1)} fusion(f32[512,32,512]{0,2,1:T(8,128)} %get-tuple-element.993, f32[512,32]{0,1:T(8,128)} %copy.76, f32[512,32]{0,1:T(8,128)} %log_add_fusion, bf16[512,32,128]{2,0,1:T(8,128)(2,1)} %convolution_convert_fusion.5, bf16[512,32,128]{2,1,0:T(8,128)(2,1)} %param.17), kind=kOutput, calls=%fused_computation.145 | convolution fusion | flops 2189426688 | bytes 58851328 | tf_op jit(solution)/shard_map/qhd,khd->qhk/dot_general | solution.py:40
  408.1 13.5 %convolution_convert_fusion.4 = bf16[32,512,128]{2,1,0:T(8,128)(2,1)} fusion(bf16[512,32,512]{0,2,1:T(8,128)(2,1)} %fusion.167, bf16[512,32,192]{0,2,1:T(8,128)(2,1)} %param.16), kind=kOutput, calls=%fused_computation.175 | convolution fusion | flops 2149580800 | bytes 25165824 | tf_op jit(solution)/shard_map/qhk,qhd->khd/dot_general | solution.py:44
  435.1 12.0 convolution_bitcast_fusion.2
  447.1 11.1 fusion.212
  458.3 12.3 convolution_bitcast_fusion.3
  493.4 461.0 %while.53 = (s32[]{:T(128)}, bf16[512,512]{1,0:T(8,128)(2,1)}, bf16[512,64]{0,1:T(8,128)(2,1)}, f32[512,32,128]{0,2,1:T(8,128)}, f32[512,32,64]{0,2,1:T(8,128)},...) while((s32[]{:T(128)}, bf16[512,512]{1,0:T(8,128)(2,1)}, ...), condition=%wide.region_14.15_spmd, body=%wide.region_11.14_spmd.sunk | while | flops 19915636736 | bytes 505349440 | solution.py:129
  495.9 19.7 %collective-permute-done.3 = bf16[512,64]{0,1:T(8,128)(2,1)S(1)} collective-permute-done((bf16[512,64]{0,1:T(8,128)(2,1)}, bf16[512,64]{0,1:T(8,128)(2,1)S(1)}, u32[]{:S(2)}, u32[]{:S(2)}) %collective-permute-start.3) | collective-permute-done | bytes 65568 | tf_op jit(solution)/shard_map/while/body/eval_jaxpr/ppermute | solution.py:113
  517.0 121.8 %conditional.5 = (f32[512,32,128]{0,2,1:T(8,128)}, f32[512,32,64]{0,2,1:T(8,128)}, f32[512,512]{1,0:T(8,128)}, f32[512,64]{0,1:T(8,128)}, f32[512,32,128]{0,2,1:T(8,128)}, /*index=5*/f32[512,32,128]{0,2,1:T(8,128)}) conditional(s32[]{:T(128)} %convert_element_type.188, (f32[512,32,128]{0,2,1:T(8,128)}, bf16[512,512]{1,0:T(8,128)(2,1)S(1)}, ...), branch_computations={%region_12.12_spmd, %region_13.13_spmd} | conditional | flops 19915636736 | bytes 497091200 | solution.py:127
  530.4 11.0 fusion.70
  542.1 12.1 fusion.67
  566.0 10.8 fusion.86
  601.9 10.6 bitcast_add_fusion.6
  648.5 19.7 %collective-permute-done.3 = bf16[512,64]{0,1:T(8,128)(2,1)S(1)} collective-permute-done((bf16[512,64]{0,1:T(8,128)(2,1)}, bf16[512,64]{0,1:T(8,128)(2,1)S(1)}, u32[]{:S(2)}, u32[]{:S(2)}) %collective-permute-start.3) | collective-permute-done | bytes 65568 | tf_op jit(solution)/shard_map/while/body/eval_jaxpr/ppermute | solution.py:113
  669.7 121.8 %conditional.5 = (f32[512,32,128]{0,2,1:T(8,128)}, f32[512,32,64]{0,2,1:T(8,128)}, f32[512,512]{1,0:T(8,128)}, f32[512,64]{0,1:T(8,128)}, f32[512,32,128]{0,2,1:T(8,128)}, /*index=5*/f32[512,32,128]{0,2,1:T(8,128)}) conditional(s32[]{:T(128)} %convert_element_type.188, (f32[512,32,128]{0,2,1:T(8,128)}, bf16[512,512]{1,0:T(8,128)(2,1)S(1)}, ...), branch_computations={%region_12.12_spmd, %region_13.13_spmd} | conditional | flops 19915636736 | bytes 497091200 | solution.py:127
  683.1 11.0 fusion.70
  694.8 12.4 fusion.67
  719.0 10.8 fusion.86
  754.8 10.6 bitcast_add_fusion.6
  801.5 19.7 %collective-permute-done.3 = bf16[512,64]{0,1:T(8,128)(2,1)S(1)} collective-permute-done((bf16[512,64]{0,1:T(8,128)(2,1)}, bf16[512,64]{0,1:T(8,128)(2,1)S(1)}, u32[]{:S(2)}, u32[]{:S(2)}) %collective-permute-start.3) | collective-permute-done | bytes 65568 | tf_op jit(solution)/shard_map/while/body/eval_jaxpr/ppermute | solution.py:113
  822.6 121.8 %conditional.5 = (f32[512,32,128]{0,2,1:T(8,128)}, f32[512,32,64]{0,2,1:T(8,128)}, f32[512,512]{1,0:T(8,128)}, f32[512,64]{0,1:T(8,128)}, f32[512,32,128]{0,2,1:T(8,128)}, /*index=5*/f32[512,32,128]{0,2,1:T(8,128)}) conditional(s32[]{:T(128)} %convert_element_type.188, (f32[512,32,128]{0,2,1:T(8,128)}, bf16[512,512]{1,0:T(8,128)(2,1)S(1)}, ...), branch_computations={%region_12.12_spmd, %region_13.13_spmd} | conditional | flops 19915636736 | bytes 497091200 | solution.py:127
  836.0 11.0 fusion.70
  847.7 12.1 fusion.67
  871.6 10.8 fusion.86
  907.4 10.6 bitcast_add_fusion.6
  954.6 15.6 %collective-permute-done.7 = f32[512,64]{0,1:T(8,128)S(1)} collective-permute-done((f32[512,64]{0,1:T(8,128)}, f32[512,64]{0,1:T(8,128)S(1)}, u32[]{:S(2)}, u32[]{:S(2)}) %collective-permute-start.7) | collective-permute-done | bytes 131104 | tf_op jit(solution)/shard_map/ppermute | solution.py:132
  971.2 10.3 copy.90
  991.7 10.5 pad_maximum_fusion.7
  1002.2 26.2 %all-reduce.7.cloned.1.call-done = (f32[512,512]{1,0:T(8,128)}, f32[512,64]{0,1:T(8,128)}) async-done(((f32[512,512]{1,0:T(8,128)}, f32[512,64]{0,1:T(8,128)}), (f32[512,512]{1,0:T(8,128)}, f32[512,64]{0,1:T(8,128)})) %all-reduce.7.cloned.1.call-update) | async-done | bytes 1179664 | tf_op jit(solution)/shard_map/psum | solution.py:135
  1028.5 290.7 %all-reduce.5.cloned.1.call-done = (f32[512,32,128]{2,1,0:T(8,128)}, f32[512,32,128]{2,1,0:T(8,128)}) async-done(((f32[512,32,128]{2,1,0:T(8,128)}, f32[512,32,128]{2,1,0:T(8,128)}), (f32[512,32,128]{2,1,0:T(8,128)}, f32[512,32,128]{2,1,0:T(8,128)})) %all-reduce.5.cloned.1.call-update) | async-done | bytes 16777232 | tf_op jit(solution)/shard_map/psum | solution.py:137
  (307 shorter events, 400.7 us)
Async XLA Ops:
  7.2 1021.3 %all-reduce.7.cloned.1.call-start = ((), (), s32[]{:S(2)}) async-start(), calls=%async_computation.1 | async-start | bytes 2359296 | tf_op jit(solution)/shard_map/psum | solution.py:135
  24.5 16.8 %copy-start.26 = (bf16[512,32,128]{2,0,1:T(8,128)(2,1)}, bf16[512,32,128]{2,0,1:T(8,128)(2,1)S(1)}, u32[]{:S(2)}) copy-start(bf16[512,32,128]{2,0,1:T(8,128)(2,1)S(1)} %convolution_convert_fusion.6) | copy-start | bytes 12582916
  68.3 13.4 copy-start.7
  131.3 10.1 collective-permute-start
  131.9 9.5 collective-permute-start.1
  200.5 9.4 collective-permute-start
  200.6 9.3 collective-permute-start.1
  269.1 9.4 collective-permute-start
  269.1 9.3 collective-permute-start.1
  458.2 12.3 copy-start.10
  481.3 8.2 copy-start.9
  481.3 8.2 copy-start.28
  493.5 23.4 %collective-permute-start.4 = (f32[512,512]{1,0:T(8,128)}, f32[512,512]{1,0:T(8,128)S(1)}, u32[]{:S(2)}, u32[]{:S(2)}) collective-permute-start(f32[512,512]{1,0:T(8,128)} %get-tuple-element.1273), channel_id=1, source_target_pairs={{0,1},{1,2},{2,3},{3,0},{4,5},{5,6},{6,7},{7,4},{8,9},{9,10},{10,1... | collective-permute-start | bytes 3145736 | tf_op jit(solution)/shard_map/while/body/eval_jaxpr/ppermute | solution.py:114
  493.6 22.6 %collective-permute-start.2 = (bf16[512,512]{1,0:T(8,128)(2,1)}, bf16[512,512]{1,0:T(8,128)(2,1)S(1)}, u32[]{:S(2)}, u32[]{:S(2)}) collective-permute-start(bf16[512,512]{1,0:T(8,128)(2,1)} %get-tuple-element.1269), channel_id=1, source_target_pairs={{0,1},{1,2},{2,3},{3,0},{4,5},{5,6},{6,7},{7,4},{8,9},{9,10},{10,1... | collective-permute-start | bytes 1572872 | tf_op jit(solution)/shard_map/while/body/eval_jaxpr/ppermute | solution.py:112
  493.7 23.3 %collective-permute-start.5 = (f32[512,64]{0,1:T(8,128)}, f32[512,64]{0,1:T(8,128)S(1)}, u32[]{:S(2)}, u32[]{:S(2)}) collective-permute-start(f32[512,64]{0,1:T(8,128)} %get-tuple-element.1274), channel_id=1, source_target_pairs={{0,1},{1,2},{2,3},{3,0},{4,5},{5,6},{6,7},{7,4},{8,9},{9,10},{10,1... | collective-permute-start | bytes 393224 | tf_op jit(solution)/shard_map/while/body/eval_jaxpr/ppermute | solution.py:115
  493.7 21.8 %collective-permute-start.3 = (bf16[512,64]{0,1:T(8,128)(2,1)}, bf16[512,64]{0,1:T(8,128)(2,1)S(1)}, u32[]{:S(2)}, u32[]{:S(2)}) collective-permute-start(bf16[512,64]{0,1:T(8,128)(2,1)} %get-tuple-element.1270), channel_id=1, source_target_pairs={{0,1},{1,2},{2,3},{3,0},{4,5},{5,6},{6,7},{7,4},{8,9},{9,10},{10,1... | collective-permute-start | bytes 196616 | tf_op jit(solution)/shard_map/while/body/eval_jaxpr/ppermute | solution.py:113
  530.4 11.7 copy-start.12
  554.3 8.4 copy-start.19
  566.0 10.8 copy-start.38
  576.8 7.8 copy-start.15
  601.9 10.6 copy-start.4
  601.9 10.6 copy-start.30
  614.6 7.4 slice-start.6
  646.2 23.4 %collective-permute-start.4 = (f32[512,512]{1,0:T(8,128)}, f32[512,512]{1,0:T(8,128)S(1)}, u32[]{:S(2)}, u32[]{:S(2)}) collective-permute-start(f32[512,512]{1,0:T(8,128)} %get-tuple-element.1273), channel_id=1, source_target_pairs={{0,1},{1,2},{2,3},{3,0},{4,5},{5,6},{6,7},{7,4},{8,9},{9,10},{10,1... | collective-permute-start | bytes 3145736 | tf_op jit(solution)/shard_map/while/body/eval_jaxpr/ppermute | solution.py:114
  646.3 22.6 %collective-permute-start.2 = (bf16[512,512]{1,0:T(8,128)(2,1)}, bf16[512,512]{1,0:T(8,128)(2,1)S(1)}, u32[]{:S(2)}, u32[]{:S(2)}) collective-permute-start(bf16[512,512]{1,0:T(8,128)(2,1)} %get-tuple-element.1269), channel_id=1, source_target_pairs={{0,1},{1,2},{2,3},{3,0},{4,5},{5,6},{6,7},{7,4},{8,9},{9,10},{10,1... | collective-permute-start | bytes 1572872 | tf_op jit(solution)/shard_map/while/body/eval_jaxpr/ppermute | solution.py:112
  646.3 23.3 %collective-permute-start.5 = (f32[512,64]{0,1:T(8,128)}, f32[512,64]{0,1:T(8,128)S(1)}, u32[]{:S(2)}, u32[]{:S(2)}) collective-permute-start(f32[512,64]{0,1:T(8,128)} %get-tuple-element.1274), channel_id=1, source_target_pairs={{0,1},{1,2},{2,3},{3,0},{4,5},{5,6},{6,7},{7,4},{8,9},{9,10},{10,1... | collective-permute-start | bytes 393224 | tf_op jit(solution)/shard_map/while/body/eval_jaxpr/ppermute | solution.py:115
  646.4 21.8 %collective-permute-start.3 = (bf16[512,64]{0,1:T(8,128)(2,1)}, bf16[512,64]{0,1:T(8,128)(2,1)S(1)}, u32[]{:S(2)}, u32[]{:S(2)}) collective-permute-start(bf16[512,64]{0,1:T(8,128)(2,1)} %get-tuple-element.1270), channel_id=1, source_target_pairs={{0,1},{1,2},{2,3},{3,0},{4,5},{5,6},{6,7},{7,4},{8,9},{9,10},{10,1... | collective-permute-start | bytes 196616 | tf_op jit(solution)/shard_map/while/body/eval_jaxpr/ppermute | solution.py:113
  683.1 11.7 copy-start.12
  707.2 8.4 copy-start.19
  719.0 10.8 copy-start.38
  729.8 7.8 copy-start.15
  754.8 10.6 copy-start.4
  754.8 10.6 copy-start.30
  799.1 23.4 %collective-permute-start.4 = (f32[512,512]{1,0:T(8,128)}, f32[512,512]{1,0:T(8,128)S(1)}, u32[]{:S(2)}, u32[]{:S(2)}) collective-permute-start(f32[512,512]{1,0:T(8,128)} %get-tuple-element.1273), channel_id=1, source_target_pairs={{0,1},{1,2},{2,3},{3,0},{4,5},{5,6},{6,7},{7,4},{8,9},{9,10},{10,1... | collective-permute-start | bytes 3145736 | tf_op jit(solution)/shard_map/while/body/eval_jaxpr/ppermute | solution.py:114
  799.2 22.6 %collective-permute-start.2 = (bf16[512,512]{1,0:T(8,128)(2,1)}, bf16[512,512]{1,0:T(8,128)(2,1)S(1)}, u32[]{:S(2)}, u32[]{:S(2)}) collective-permute-start(bf16[512,512]{1,0:T(8,128)(2,1)} %get-tuple-element.1269), channel_id=1, source_target_pairs={{0,1},{1,2},{2,3},{3,0},{4,5},{5,6},{6,7},{7,4},{8,9},{9,10},{10,1... | collective-permute-start | bytes 1572872 | tf_op jit(solution)/shard_map/while/body/eval_jaxpr/ppermute | solution.py:112
  799.3 23.3 %collective-permute-start.5 = (f32[512,64]{0,1:T(8,128)}, f32[512,64]{0,1:T(8,128)S(1)}, u32[]{:S(2)}, u32[]{:S(2)}) collective-permute-start(f32[512,64]{0,1:T(8,128)} %get-tuple-element.1274), channel_id=1, source_target_pairs={{0,1},{1,2},{2,3},{3,0},{4,5},{5,6},{6,7},{7,4},{8,9},{9,10},{10,1... | collective-permute-start | bytes 393224 | tf_op jit(solution)/shard_map/while/body/eval_jaxpr/ppermute | solution.py:115
  799.3 21.8 %collective-permute-start.3 = (bf16[512,64]{0,1:T(8,128)(2,1)}, bf16[512,64]{0,1:T(8,128)(2,1)S(1)}, u32[]{:S(2)}, u32[]{:S(2)}) collective-permute-start(bf16[512,64]{0,1:T(8,128)(2,1)} %get-tuple-element.1270), channel_id=1, source_target_pairs={{0,1},{1,2},{2,3},{3,0},{4,5},{5,6},{6,7},{7,4},{8,9},{9,10},{10,1... | collective-permute-start | bytes 196616 | tf_op jit(solution)/shard_map/while/body/eval_jaxpr/ppermute | solution.py:113
  836.0 11.7 copy-start.12
  859.8 8.4 copy-start.19
  871.6 10.8 copy-start.38
  882.4 7.8 copy-start.15
  907.4 10.6 copy-start.4
  907.4 10.6 copy-start.30
  954.4 15.7 %collective-permute-start.6 = (f32[512,512]{1,0:T(8,128)}, f32[512,512]{1,0:T(8,128)S(1)}, u32[]{:S(2)}, u32[]{:S(2)}) collective-permute-start(f32[512,512]{1,0:T(8,128)} %get-tuple-element.878), channel_id=1, source_target_pairs={{0,1},{1,2},{2,3},{3,0},{4,5},{5,6},{6,7},{7,4},{8,9},{9,10},{10,1... | collective-permute-start | bytes 3145736 | tf_op jit(solution)/shard_map/ppermute | solution.py:131
  954.5 15.6 %collective-permute-start.7 = (f32[512,64]{0,1:T(8,128)}, f32[512,64]{0,1:T(8,128)S(1)}, u32[]{:S(2)}, u32[]{:S(2)}) collective-permute-start(f32[512,64]{0,1:T(8,128)} %get-tuple-element.879), channel_id=1, source_target_pairs={{0,1},{1,2},{2,3},{3,0},{4,5},{5,6},{6,7},{7,4},{8,9},{9,10},{10,1... | collective-permute-start | bytes 393224 | tf_op jit(solution)/shard_map/ppermute | solution.py:132
  971.1 348.0 %all-reduce.5.cloned.1.call-start = ((), (), s32[]{:S(2)}) async-start(), calls=%async_computation | async-start | bytes 33554432 | tf_op jit(solution)/shard_map/psum | solution.py:137
  1321.4 9.7 slice-start.10
  1323.1 7.9 slice-start.11
  (50 other events, 188.9 us)
Sparse Core Ops, SparseCore 0:
  971.3 57.1 all-reduce.6
  1031.7 287.4 all-reduce.4
where the time goes:
time: 1350 us; the launch traced here: 1340 us
  matrix products  577 us (43%)
  waiting for transfers between devices  417 us (31%)
  local copies, waits for them, and re-layouts  136 us (10%)
  other arithmetic  104 us (8%)
  loops' own time  82.5 us (6%)
  between operations  14.4 us (1%)
    psum x1, waiting for transfers between devices, device_fn(): lax.psum(dw_k, 'cp')  291 us
    dot_general x7, matrix products, block_scores(): jnp.einsum('qhd,kd->qhk', q_rope, rope_blk, preferred_element_type=jnp.fl...  92 us
    dot_general x7, matrix products, block_scores(): jnp.einsum('qhd,khd->qhk', q_nope, knope_blk, preferred_element_type=jnp....  70.1 us
    dot_general x4, matrix products, forward_update(): jnp.einsum('qhk,khd->qhd', prob_blk.astype(jnp.bfloat16), v_blk, preferre...  67.8 us
    ppermute x3, waiting for transfers between devices, backward_hop(): rope_blk = lax.ppermute(rope_blk, 'cp', shift_perm)  59.1 us
    dot_general x4, matrix products, backward_block(): jnp.einsum('qhd,khd->qhk', d_out, v_blk, preferred_element_type=jnp.float32)  58.6 us
    dot_general x4, matrix products, backward_block(): jnp.einsum('qhk,qhd->khd', prob_blk.astype(jnp.bfloat16), d_out, preferre...  52.4 us
    unnamed x39, local copies, waits for them, and re-layouts  43.4 us
  transfers between devices with their start and end apart: 22, of which 9 were waited for; matrix products, arithmetic and copies ran while one was open for 3% of the time, Pallas kernels for 0%

commit v1 on v0

v1 whole, which is shorter than its diff:
```python
import functools
import jax
import jax.numpy as jnp
from jax import lax
from jax.experimental import pallas as pl
from jax.experimental.pallas import tpu as pltpu
from jax.sharding import PartitionSpec as P

NEG_BIG = -1.0e30
LOG2E = 1.4426950408889634
F32 = jnp.float32
BF16 = jnp.bfloat16
CHUNKS = (8, 8, 8, 8)
POST = 'mid'


def mm(a, b):
    return jnp.dot(a, b, preferred_element_type=F32)


def mm_nt(a, b):
    return lax.dot_general(a, b, (((1,), (1,)), ((), ())), preferred_element_type=F32)


def attn_body(n_cp, half, scale, first, n_h, *refs):
    n_blk = n_cp
    c_refs, rt_refs = refs[:n_blk], refs[n_blk:2 * n_blk]
    qt_ref, do_ref, wk_ref, wv_ref, wk_old, wv_old = refs[2 * n_blk:2 * n_blk + 6]
    rest = refs[2 * n_blk + 6:]
    if not first:
        keep_in, send_in = rest[0], rest[1]
        rest = rest[4:]
    (ot_ref, dqt_ref, keep_ref, send_ref, dwk_ref, dws_ref,
     ct, kk, kt, v_s, vt_s, p_s, dkv, dr_s, o_s, dq_s, q_s, qt_s, dot_s, bias, dw_s) = rest
    h = pl.program_id(0)
    me = lax.axis_index('cp')
    d_nope = do_ref.shape[2]
    d_qk = qt_ref.shape[1]
    d_rope = d_qk - d_nope
    blk, _ = c_refs[0].shape
    keys = blk * n_blk
    n_t = 2 * n_cp + 1
    c2 = scale * LOG2E
    acc_refs = [(keep_ref, 0), (send_ref, 0), (keep_ref, 1), (send_ref, 1)]
    even = lax.rem(me, 2) == 0

    @pl.when(h == 0)
    def _():
        for j in range(n_blk):
            rows = slice(j * blk, (j + 1) * blk)
            ct[:, rows] = c_refs[j][...].T
            rt = rt_refs[j][...]
            kt[d_nope:, rows] = rt
            kk[rows, d_nope:] = jnp.concatenate([rt, jnp.zeros((128 - d_rope, blk), BF16)], axis=0).T
        qt_s[d_qk:, :] = jnp.zeros((qt_s.shape[0] - d_qk, qt_s.shape[1]), BF16)
        dr_s[...] = jnp.zeros_like(dr_s)
        dkv[...] = jnp.zeros_like(dkv)
        k_io = lax.broadcasted_iota(jnp.int32, (half, half), 0)
        q_io = lax.broadcasted_iota(jnp.int32, (half, half), 1)
        bias[0] = jnp.zeros((half, half), F32)
        bias[1] = jnp.where(k_io <= q_io, 0.0, NEG_BIG)
        if first:
            keep_ref[...] = jnp.zeros_like(keep_ref)
            send_ref[...] = jnp.zeros_like(send_ref)
        else:
            keep_ref[...] = keep_in[...]
            send_ref[...] = send_in[...]

    def post(j, w):
        rows = slice(j * half, (j + 1) * half)
        g = dkv[rows, :].astype(BF16)
        ref, i = acc_refs[j // 2]
        part = mm(ct[:, rows], g)
        dw_s[...] = part if j == 0 else dw_s[...] + part
        o = j % 2 * half
        ref[i, o:o + half, :] += mm_nt(g, w)
        dkv[rows, :] = jnp.zeros((half, dkv.shape[1]), F32)

    def post_out():
        dwk, dwv = dw_s[:, :d_nope], dw_s[:, d_nope:]
        dwk_ref[0] = jnp.where(even, dwk, dwv)
        dws_ref[0] = jnp.where(even, dwv, dwk)

    @pl.when(h < n_h)
    def _():
        w = jnp.concatenate([wk_ref[0], wv_ref[0]], axis=1)
        w_old = jnp.concatenate([wk_old[0], wv_old[0]], axis=1)
        for j in range(0, keys, half):
            rows = slice(j, j + half)
            kv = mm(c_refs[j // blk][j % blk:j % blk + half, :], w).astype(BF16)
            kk[rows, :d_nope] = kv[:, :d_nope]
            v_s[rows, :] = kv[:, d_nope:]
            kt[:d_nope, rows] = kv[:, :d_nope].T
            vt_s[:, rows] = kv[:, d_nope:].T
        qt_s[:d_qk, :] = qt_ref[0]
        q_s[...] = qt_s[...].T
        dot_s[...] = do_ref[0].T

        tiles = []
        for t in range(n_t):
            if t == 0:
                is_a, qo, kp = True, 0, 0
            elif t < n_cp:
                is_a = t <= me
                qo = pl.multiple_of(jnp.where(is_a, 0, half), half)
                kp = jnp.where(is_a, t, t - me - 1)
            else:
                is_a, qo, kp = None, half, t - me - 1
            low = kp < n_cp
            owner = jnp.where(low, kp, 2 * n_cp - 1 - kp)
            ko = pl.multiple_of(jnp.bitwise_xor(owner, me) * blk + jnp.where(low, 0, half), half)
            tiles.append((t, is_a, qo, ko))

        def pick(is_a, a, b):
            return b if is_a is None else a if is_a is True else jnp.where(is_a, a, b)

        def put(is_a, cur, new):
            a, b = cur
            if is_a is True:
                return (new, b)
            if is_a is None:
                return (a, new)
            return (jnp.where(is_a, new, a), jnp.where(is_a, b, new))

        neg = jnp.full((1, half), NEG_BIG, F32)
        zero = jnp.zeros((1, half), F32)
        m, l = (neg, neg), (zero, zero)
        for t, is_a, qo, ko in tiles:
            s = mm(kk[pl.ds(ko, half), :], qt_s[:, pl.ds(qo, half)])
            if t == n_t - 1:
                s = s + bias[1]
            elif t < n_cp:
                s = s + bias[jnp.where(t == me, 1, 0)]
            p_s[t] = s
            m = put(is_a, m, jnp.maximum(pick(is_a, *m), jnp.max(s, axis=0, keepdims=True)))
        m = tuple(x * c2 for x in m)
        acc_o = None
        for t, is_a, qo, ko in tiles:
            p = jnp.exp2(p_s[t] * c2 - pick(is_a, *m))
            l = put(is_a, l, pick(is_a, *l) + jnp.sum(p, axis=0, keepdims=True))
            p_s[t] = p
            o = mm(vt_s[:, pl.ds(ko, half)], p.astype(BF16))
            if t == 0:
                o_s[:, :half] = o
                o_s[:, half:] = jnp.zeros_like(o)
            elif t < n_cp:
                o_s[:, pl.ds(qo, half)] += o
            else:
                acc_o = o if acc_o is None else acc_o + o
            if POST == 'mid' and t < 2 * n_blk:
                post(t, w_old)
        o_s[:, half:] += acc_o
        if POST == 'mid':
            post_out()
        linv = tuple(1.0 / x for x in l)
        dd = []
        for i in range(2):
            cols = slice(i * half, (i + 1) * half)
            o = o_s[:, cols] * linv[i]
            ot_ref[0, :, cols] = o.astype(BF16)
            dd.append(jnp.sum(o * dot_s[:, cols].astype(F32), axis=0, keepdims=True))

        acc_q = None
        for t, is_a, qo, ko in tiles:
            p = p_s[t] * (pick(is_a, *linv))
            rows = pl.ds(ko, half)
            dp = mm(v_s[rows, :], dot_s[:, pl.ds(qo, half)])
            ds = (p * (dp - pick(is_a, *dd))).astype(BF16)
            dv = mm(p.astype(BF16), do_ref[0, pl.ds(qo, half), :])
            dk = mm(ds, q_s[pl.ds(qo, half), :]) * scale
            dq = mm(kt[:, rows], ds)
            dkv[rows, :d_nope] += dk[:, :d_nope]
            dkv[rows, d_nope:] += dv
            dr_s[rows, :] += dk[:, d_nope:]
            if t == 0:
                dq_s[:, :half] = dq
                dq_s[:, half:] = jnp.zeros_like(dq)
            elif t < n_cp:
                dq_s[:, pl.ds(qo, half)] += dq
            else:
                acc_q = dq if acc_q is None else acc_q + dq
        dqt_ref[0, :, :half] = dq_s[:, :half] * scale
        dqt_ref[0, :, half:] = (dq_s[:, half:] + acc_q) * scale

    @pl.when(h == n_h)
    def _():
        w_old = jnp.concatenate([wk_old[0], wv_old[0]], axis=1)
        for j in range(2 * n_blk):
            post(j, w_old)
        for j in range(n_blk):
            ref, i = acc_refs[j]
            ref[i, blk:, :] += dr_s[j * blk:(j + 1) * blk, :].T[:d_rope, :]
        post_out()


def attn_call(n_cp, scale, h0, n_h, cs, rts, qt, do_h, wk_h, wv_h, carry):
    heads, d_qk, rows = qt.shape
    blk, rank = cs[0].shape
    d_rope = rts[0].shape[0]
    keys = blk * n_cp
    d_val = do_h.shape[2]
    half = rows // 2
    n_t = 2 * n_cp + 1
    first = carry is None
    full = lambda *shape: pl.BlockSpec(shape, lambda h: (0,) * len(shape))
    head = lambda *shape: pl.BlockSpec((1,) + shape, lambda h: (jnp.minimum(h, n_h - 1) + h0,) + (0,) * len(shape))
    prev = lambda *shape: pl.BlockSpec((1,) + shape, lambda h: (jnp.maximum(h - 1, 0) + h0,) + (0,) * len(shape))
    local = lambda *shape: pl.BlockSpec((1,) + shape, lambda h: (jnp.maximum(h - 1, 0),) + (0,) * len(shape))
    in_specs = [full(blk, rank)] * n_cp + [full(d_rope, blk)] * n_cp + [
        head(d_qk, rows), head(rows, d_val), head(rank, d_val), head(rank, d_val),
        prev(rank, d_val), prev(rank, d_val)]
    args = [*cs, *rts, qt, do_h, wk_h, wv_h, wk_h, wv_h]
    aliases = {}
    acc = (2, blk + d_rope, rank)
    if not first:
        ot, dqt, keep, send = carry
        n = len(args)
        in_specs += [full(*acc), full(*acc), pl.BlockSpec(memory_space=pl.ANY), pl.BlockSpec(memory_space=pl.ANY)]
        args += [keep, send, ot, dqt]
        aliases = {n + 2: 0, n + 3: 1}
    out_shape = [jax.ShapeDtypeStruct((heads, d_val, rows), BF16),
                 jax.ShapeDtypeStruct((heads, d_qk, rows), F32),
                 jax.ShapeDtypeStruct(acc, F32),
                 jax.ShapeDtypeStruct(acc, F32),
                 jax.ShapeDtypeStruct((n_h, rank, d_val), F32),
                 jax.ShapeDtypeStruct((n_h, rank, d_val), F32)]
    out_specs = [head(d_val, rows), head(d_qk, rows), full(*acc), full(*acc), local(rank, d_val), local(rank, d_val)]
    scratch = [pltpu.VMEM((rank, keys), BF16),
               pltpu.VMEM((keys, 256), BF16), pltpu.VMEM((d_qk, keys), BF16),
               pltpu.VMEM((keys, d_val), BF16), pltpu.VMEM((d_val, keys), BF16),
               pltpu.VMEM((n_t, half, half), F32),
               pltpu.VMEM((keys, 2 * d_val), F32), pltpu.VMEM((keys, 128), F32),
               pltpu.VMEM((d_val, rows), F32), pltpu.VMEM((d_qk, rows), F32),
               pltpu.VMEM((rows, 256), BF16), pltpu.VMEM((256, rows), BF16),
               pltpu.VMEM((d_val, rows), BF16), pltpu.VMEM((2, half, half), F32), pltpu.VMEM((rank, 2 * d_val), F32)]
    flops = n_h * (3 * 2 * keys * rank * 2 * d_val + n_t * half * half * 2 * 1024)
    return pl.pallas_call(
        functools.partial(attn_body, n_cp, half, scale, first, n_h),
        grid=(n_h + 1,), in_specs=in_specs, out_specs=out_specs, out_shape=out_shape,
        scratch_shapes=scratch, input_output_aliases=aliases,
        compiler_params=pltpu.CompilerParams(dimension_semantics=("arbitrary",), vmem_limit_bytes=60 * 2**20),
        cost_estimate=pl.CostEstimate(flops=flops, bytes_accessed=n_h * 2**20, transcendentals=0),
        name="attn",
    )(*args)


def place_body(sizes, *refs):
    n = len(sizes)
    mine, other = refs[:n], refs[n:2 * n]
    k_ref, v_ref = refs[-2:]
    even = lax.rem(lax.axis_index('cp'), 2) == 0
    o = 0
    for i, n_h in enumerate(sizes):
        for j in range(n_h):
            a, b = mine[i][j], other[i][j]
            k_ref[:, o, :] = jnp.where(even, a, b)
            v_ref[:, o, :] = jnp.where(even, b, a)
            o += 1


def place(group, heads, mine, other, carry):
    sizes = [x.shape[0] for x in mine]
    n_g = sum(sizes)
    _, rank, d_val = mine[0].shape
    step = 128
    ins = [pl.BlockSpec((n_h, step, d_val), lambda r: (0, r, 0)) for n_h in sizes] * 2
    args = [*mine, *other]
    aliases = {}
    if carry is not None:
        aliases = {len(args): 0, len(args) + 1: 1}
        args += list(carry)
        ins = ins + [pl.BlockSpec(memory_space=pl.ANY)] * 2
    out = jax.ShapeDtypeStruct((rank, heads, d_val), F32)
    return pl.pallas_call(
        functools.partial(place_body, sizes), grid=(rank // step,), in_specs=ins,
        out_specs=[pl.BlockSpec((step, n_g, d_val), lambda r: (r, group, 0))] * 2,
        out_shape=[out, out], input_output_aliases=aliases,
        compiler_params=pltpu.CompilerParams(dimension_semantics=("arbitrary",)),
        cost_estimate=pl.CostEstimate(flops=10 ** 9, bytes_accessed=4 * n_g * rank * d_val * 4, transcendentals=0),
        name="place",
    )(*args)


def swap(x, axis, size, bit):
    return lax.ppermute(x, axis, [(i, i ^ bit) for i in range(size)])


def solution(mesh):
    n_cp = mesh.shape['cp']
    seq_spec = P(('dp', 'cp'), None)
    head_spec = P(('dp', 'cp'), 'tp', None)
    weight_spec = P(None, 'tp', None)
    grad_spec = P('dp', 'tp', None)

    def device_body(c_latent, k_rope, q_heads, d_out, w_uk, w_uv):
        rows = c_latent.shape[0]
        scale = q_heads.shape[2] ** -0.5
        heads = q_heads.shape[1]
        n_tp = mesh.shape['tp']
        rt = k_rope.T
        c2, r2 = swap(c_latent, 'cp', n_cp, 2), swap(rt, 'cp', n_cp, 2)
        c1, r1 = swap(c_latent, 'cp', n_cp, 1), swap(rt, 'cp', n_cp, 1)
        c3, r3 = swap(c2, 'cp', n_cp, 1), swap(r2, 'cp', n_cp, 1)
        cs, rts = (c_latent, c1, c2, c3), (rt, r1, r2, r3)
        qt = jnp.transpose(q_heads, (1, 2, 0))
        do_h = jnp.transpose(d_out, (1, 0, 2))
        wk_h = jnp.transpose(w_uk, (1, 0, 2))
        wv_h = jnp.transpose(w_uv, (1, 0, 2))
        carry = None
        h0 = 0
        mine, other = [], []
        placed = None
        for n_h in CHUNKS:
            *carry, dw_keep, dw_send = attn_call(n_cp, scale, h0, n_h, cs, rts, qt, do_h, wk_h, wv_h, carry)
            h0 += n_h
            chip = dw_keep + swap(dw_send, 'cp', n_cp, 1)
            far = swap(chip, 'cp', n_cp, 2)
            total = chip + far
            mine.append(total)
            other.append(swap(total, 'cp', n_cp, 1))
            if h0 % 8 == 0:
                placed = place(h0 // 8 - 1, heads, mine, other, placed)
                mine, other = [], []
        ot, dqt, keep, send = carry
        chip = keep + swap(send, 'cp', n_cp, 1)
        acc = chip[0] + swap(chip[1], 'cp', n_cp, 2)
        odd = lax.rem(lax.axis_index('tp'), 2) == 1
        outs = []
        cols = acc.shape[1] // 2
        for i in range(2):
            x = acc[:, i * cols:(i + 1) * cols]
            mid = x.shape[0] // 2
            lo, hi = x[:mid], x[mid:]
            x = jnp.where(odd, hi, lo) + swap(jnp.where(odd, lo, hi), 'tp', n_tp, 1)
            x = x + swap(x, 'tp', n_tp, 2)
            y = swap(x, 'tp', n_tp, 1)
            outs.append(jnp.concatenate([jnp.where(odd, y, x), jnp.where(odd, x, y)], axis=0))
        acc = jnp.concatenate(outs, axis=1)
        return (jnp.transpose(ot, (2, 0, 1)), jnp.transpose(dqt, (2, 0, 1)), acc[:rows], acc[rows:].T, placed[0], placed[1])

    return jax.shard_map(device_body, mesh=mesh,
                         in_specs=(seq_spec, seq_spec, head_spec, head_spec, weight_spec, weight_spec),
                         out_specs=(head_spec, head_spec, seq_spec, seq_spec, grad_spec, grad_spec),
                         check_vma=False)
```

time: 1350 us -> 528 us (0.39)
  matrix products: 577 us -> 0 us
  Pallas kernels: 0 us -> 203 us
  waiting for transfers between devices: 417 us -> 254 us
  local copies, waits for them, and re-layouts: 136 us -> 22.7 us
  loops' own time: 82.5 us -> 0 us
  other arithmetic: 104 us -> 22.8 us
    dot_general x63 -> x0, matrix products: 577 us -> none  [the longest x7 92 us: block_scores(): jnp.einsum('qhd,kd->qhk', q_rope, rope_blk, preferred_element_type=jnp.fl...]
    psum x2 -> x0, waiting for transfers between devices: 317 us -> none  [the longest x1 291 us: device_fn(): lax.psum(dw_k, 'cp')]
    pallas_call x0 -> x8, Pallas kernels: none -> 203 us  [the longest x4 180 us: attn_call(): pl.pallas_call(functools.partial(attn_body, n_cp, half, scale, first, n_h...]
    ppermute x20 -> x26, waiting for transfers between devices: 100 us -> 254 us  [swap(): return lax.ppermute(x, axis, [(i, i ^ bit) for i in range(size)])]
    another operation x8 -> x0, loops' own time: 82.5 us -> none  [the longest x3 29.5 us: backward_hop(): lax.cond(src_idx < my_idx, earlier_keys, later_queries, acc_mid)]
    concatenate x14 -> x1, other arithmetic: 54.2 us -> 0.16 us  [device_body(): acc = jnp.concatenate(outs, axis=1)]
    reduce_sum x5 -> x0, other arithmetic: 48.5 us -> none  [the longest x4 39.6 us: forward_update(): new_sum = run_sum * rescale + jnp.sum(prob_blk, axis=-1)]
    while x19 -> x0, local copies, waits for them, and re-layouts: 37.8 us -> none  [the longest x2 20.5 us: device_fn(): lax.fori_loop(1, n_cp, backward_hop, (c_latent, k_rope, grad_acc))[2]]
  transfers between devices with their start and end apart: 22 -> 26, of which waited for: 9 -> 9; matrix products, arithmetic and copies ran while one was open for 3% -> 9% of each run, Pallas kernels for 0% -> 3%
where the time goes in v1:
time: 528 us; the launch traced here: 520 us
  waiting for transfers between devices  254 us (48%)
  Pallas kernels  203 us (38%)
  other arithmetic  22.8 us (4%)
  local copies, waits for them, and re-layouts  22.7 us (4%)
  starting transfers between devices  16.1 us (3%)
    ppermute x26, waiting for transfers between devices, swap(): return lax.ppermute(x, axis, [(i, i ^ bit) for i in range(size)])  254 us
    pallas_call x4, Pallas kernels, attn_call(): pl.pallas_call(functools.partial(attn_body, n_cp, half, scale, first, n_h...  180 us
    pallas_call x4, Pallas kernels, place(): pl.pallas_call(functools.partial(place_body, sizes), grid=(rank // step,)...  22.7 us
    ppermute x26, starting transfers between devices, swap(): return lax.ppermute(x, axis, [(i, i ^ bit) for i in range(size)])  16.1 us
    add x4, other arithmetic, device_body(): total = chip + far  14.5 us
    unnamed x28, local copies, waits for them, and re-layouts  12.7 us
  transfers between devices with their start and end apart: 26, of which 9 were waited for; matrix products, arithmetic and copies ran while one was open for 9% of the time, Pallas kernels for 3%

profile of v1, /device:TPU:0, one launch (start us, length us, event | category | flops | bytes accessed | tf_op | source)
XLA Modules:
  0.0 519.7 jit_solution(3360007266578908507)
XLA Ops:
  0.6 3.1 collective-permute-start.1
  3.8 0.5 collective-permute-start.3
  4.3 12.9 %collective-permute-done.4.refs_6_ = bf16[64,512]{1,0:T(8,128)(2,1)S(1)} collective-permute-done((bf16[64,512]{1,0:T(8,128)(2,1)}, bf16[64,512]{1,0:T(8,128)(2,1)S(1)}, u32[]{:S(2)}, u32[]{:S(2)}) %collective-permute-start.4) | collective-permute-done | bytes 65568 | tf_op jit(solution)/shard_map/ppermute | solution.py:285
  17.3 0.5 collective-permute-start.2
  17.8 7.9 %copy_bitcast_fusion = (bf16[32,512,128]{2,1,0:T(8,128)(2,1)}, bf16[32,512,128]{2,1,0:T(8,128)(2,1)}) fusion(bf16[512,32,128]{2,1,0:T(8,128)(2,1)} %param.11, bf16[512,32,128]{2,1,0:T(8,128)(2,1)} %param.10), kind=kLoop, calls=%fused_computation | loop fusion | bytes 16777216 | tf_op jit(solution)/shard_map/transpose | solution.py:308
  25.6 3.6 copy.31
  29.3 0.6 copy-done.11
  30.3 43.6 %attn.4 = (bf16[32,128,512]{2,1,0:T(8,128)(2,1)}, f32[32,192,512]{2,1,0:T(8,128)}, f32[2,576,512]{2,1,0:T(8,128)}, f32[2,576,512]{2,1,0:T(8,128)}, f32[8,512,128]{2,1,0:T(8,128)}, /*index=5*/f32[8,512,128]{2,1,0:T(8,128)}) custom-call(bf16[512,512]{1,0:T(8,128)(2,1)} %refs_0_.7, bf16[512,512]{1,0:T(8,128)(2,1)} %copy-done.8, bf16[512,512]{1,0:T(8,128)(2,1)} %copy-done.7, ...), custom_call_target="tpu_custom_call" | custom-call | flops 22548578304 | bytes 8388608 | tf_op jit(solution)/shard_map/attn/pallas_call | solution.py:237
  73.9 45.5 %attn.5 = (bf16[32,128,512]{2,1,0:T(8,128)(2,1)}, f32[32,192,512]{2,1,0:T(8,128)}, f32[2,576,512]{2,1,0:T(8,128)}, f32[2,576,512]{2,1,0:T(8,128)}, f32[8,512,128]{2,1,0:T(8,128)}, /*index=5*/f32[8,512,128]{2,1,0:T(8,128)}) custom-call(bf16[512,512]{1,0:T(8,128)(2,1)} %refs_0_.7, ...), custom_call_target="tpu_custom_call", output_to_operand_aliasing={{0}: (16, {}), {1}: (17, {})} | custom-call | flops 22548578304 | bytes 8388608 | tf_op jit(solution)/shard_map/attn/pallas_call | solution.py:237
  119.4 45.3 %attn.6 = (bf16[32,128,512]{2,1,0:T(8,128)(2,1)}, f32[32,192,512]{2,1,0:T(8,128)}, f32[2,576,512]{2,1,0:T(8,128)}, f32[2,576,512]{2,1,0:T(8,128)}, f32[8,512,128]{2,1,0:T(8,128)}, /*index=5*/f32[8,512,128]{2,1,0:T(8,128)}) custom-call(bf16[512,512]{1,0:T(8,128)(2,1)} %refs_0_.7, ...), custom_call_target="tpu_custom_call", output_to_operand_aliasing={{0}: (16, {}), {1}: (17, {})} | custom-call | flops 22548578304 | bytes 8388608 | tf_op jit(solution)/shard_map/attn/pallas_call | solution.py:237
  164.8 45.6 %attn.7 = (bf16[32,128,512]{2,1,0:T(8,128)(2,1)}, f32[32,192,512]{2,1,0:T(8,128)}, f32[2,576,512]{2,1,0:T(8,128)}, f32[2,576,512]{2,1,0:T(8,128)}, f32[8,512,128]{2,1,0:T(8,128)}, /*index=5*/f32[8,512,128]{2,1,0:T(8,128)}) custom-call(bf16[512,512]{1,0:T(8,128)(2,1)} %refs_0_.7, ...), custom_call_target="tpu_custom_call", output_to_operand_aliasing={{0}: (16, {}), {1}: (17, {})} | custom-call | flops 22548578304 | bytes 8388608 | tf_op jit(solution)/shard_map/attn/pallas_call | solution.py:237
  210.5 0.5 collective-permute-start.23
  211.0 0.4 collective-permute-start.17
  211.6 6.6 %collective-permute-done.23 = f32[8,512,128]{2,1,0:T(8,128)S(1)} collective-permute-done((f32[8,512,128]{2,1,0:T(8,128)}, f32[8,512,128]{2,1,0:T(8,128)S(1)}, u32[]{:S(2)}, u32[]{:S(2)}) %collective-permute-start.23) | collective-permute-done | bytes 2097184 | tf_op jit(solution)/shard_map/ppermute | solution.py:285
  218.2 1.6 add.54
  219.8 1.0 collective-permute-start.24
  220.8 0.4 collective-permute-done.14
  221.2 1.5 add.48
  222.7 1.0 collective-permute-start.15
  223.7 0.5 collective-permute-done.17
  224.2 1.6 add.50
  225.8 1.0 collective-permute-start.18
  226.8 0.4 collective-permute-done.20
  227.2 1.5 add.52
  228.7 1.0 collective-permute-start.21
  229.7 0.5 add.42
  230.3 1.1 slice_bitcast_fusion
  231.4 1.0 collective-permute-start.7
  232.4 195.4 %collective-permute-done.7 = f32[576,512]{1,0:T(8,128)S(1)} collective-permute-done((f32[576,512]{1,0:T(8,128)}, f32[576,512]{1,0:T(8,128)S(1)}, u32[]{:S(2)}, u32[]{:S(2)}) %collective-permute-start.7) | collective-permute-done | bytes 1179680 | tf_op jit(solution)/shard_map/ppermute | solution.py:285
  427.8 0.2 fusion
  428.2 1.9 collective-permute-start.8
  430.3 3.8 add.55.refs_0_
  434.1 3.7 add.53.refs_0_
  437.8 0.5 collective-permute-start.22
  438.3 2.4 add.49.refs_0_
  440.8 4.5 add.51.refs_0_
  445.5 2.9 collective-permute-start.12
  448.4 14.0 %collective-permute-done.12 = f32[288,256]{1,0:T(8,128)S(1)} collective-permute-done((f32[288,256]{1,0:T(8,128)S(1)}, f32[288,256]{1,0:T(8,128)S(1)}, u32[]{:S(2)}, u32[]{:S(2)}) %collective-permute-start.12) | collective-permute-done | bytes 294944 | tf_op jit(solution)/shard_map/ppermute | solution.py:285
  462.4 15.9 %collective-permute-done.9 = f32[288,256]{1,0:T(8,128)S(1)} collective-permute-done((f32[288,256]{1,0:T(8,128)S(1)}, f32[288,256]{1,0:T(8,128)S(1)}, u32[]{:S(2)}, u32[]{:S(2)}) %collective-permute-start.9) | collective-permute-done | bytes 294944 | tf_op jit(solution)/shard_map/ppermute | solution.py:285
  478.4 7.8 %collective-permute-done.13 = f32[288,256]{1,0:T(8,128)S(1)} collective-permute-done((f32[288,256]{1,0:T(8,128)S(1)}, f32[288,256]{1,0:T(8,128)S(1)}, u32[]{:S(2)}, u32[]{:S(2)}) %collective-permute-start.13) | collective-permute-done | bytes 294944 | tf_op jit(solution)/shard_map/ppermute | solution.py:285
  486.2 0.3 collective-permute-start.10
  486.5 8.1 %copy.27 = bf16[512,32,128]{2,1,0:T(8,128)(2,1)} copy(bf16[512,32,128]{0,2,1:T(8,128)(2,1)} %bitcast.23) | data formatting | bytes 8388608
  494.8 1.0 slice.44
  495.9 0.7 maximum_bitcast_fusion
  496.5 5.7 %place.4 = (f32[512,32,128]{2,1,0:T(8,128)}, f32[512,32,128]{2,1,0:T(8,128)}) custom-call(f32[8,512,128]{2,1,0:T(8,128)} %add.55.refs_0_, f32[8,512,128]{2,1,0:T(8,128)} %collective-permute-done.25.refs_1_), custom_call_target="tpu_custom_call" | custom-call | flops 1000000000 | bytes 8388608 | tf_op jit(solution)/shard_map/place/pallas_call | solution.py:274
  502.2 5.7 %place.5 = (f32[512,32,128]{2,1,0:T(8,128)}, f32[512,32,128]{2,1,0:T(8,128)}) custom-call(f32[8,512,128]{2,1,0:T(8,128)} %add.53.refs_0_, f32[8,512,128]{2,1,0:T(8,128)} %collective-permute-done.22.refs_1_, f32[512,32,128]{2,1,0:T(8,128)} %get-tuple-element.62.refs_2_, ...), custom_call_target="tpu_custom_call", output_to_operand_aliasing={{0}: (2, {}), {1}: (3, {})} | custom-call | flops 1000000000 | bytes 8388608 | tf_op jit(solution)/shard_map/place/pallas_call | solution.py:274
  507.9 5.7 %place.6 = (f32[512,32,128]{2,1,0:T(8,128)}, f32[512,32,128]{2,1,0:T(8,128)}) custom-call(f32[8,512,128]{2,1,0:T(8,128)} %add.51.refs_0_, f32[8,512,128]{2,1,0:T(8,128)} %collective-permute-done.19.refs_1_, f32[512,32,128]{2,1,0:T(8,128)} %get-tuple-element.64.refs_2_, ...), custom_call_target="tpu_custom_call", output_to_operand_aliasing={{0}: (2, {}), {1}: (3, {})} | custom-call | flops 1000000000 | bytes 8388608 | tf_op jit(solution)/shard_map/place/pallas_call | solution.py:274
  513.5 5.7 %place.7 = (f32[512,32,128]{2,1,0:T(8,128)}, f32[512,32,128]{2,1,0:T(8,128)}) custom-call(f32[8,512,128]{2,1,0:T(8,128)} %copy-done, f32[8,512,128]{2,1,0:T(8,128)} %collective-permute-done.16.refs_1_, f32[512,32,128]{2,1,0:T(8,128)} %get-tuple-element.66.refs_2_, ...), custom_call_target="tpu_custom_call", output_to_operand_aliasing={{0}: (2, {}), {1}: (3, {})} | custom-call | flops 1000000000 | bytes 8388608 | tf_op jit(solution)/shard_map/place/pallas_call | solution.py:274
  (61 shorter events, 1.6 us)
Async XLA Ops:
  0.6 16.6 %collective-permute-start.1 = (bf16[512,512]{1,0:T(8,128)(2,1)}, bf16[512,512]{1,0:T(8,128)(2,1)S(1)}, u32[]{:S(2)}, u32[]{:S(2)}) collective-permute-start(bf16[512,512]{1,0:T(8,128)(2,1)} %refs_0_.7), channel_id=1, source_target_pairs={{0,2},{1,3},{2,0},{3,1},{4,6},{5,7},{6,4},{7,5},{8,10},{9,11},{10,... | collective-permute-start | bytes 1572872 | tf_op jit(solution)/shard_map/ppermute | solution.py:285
  3.7 13.5 %collective-permute-start.4 = (bf16[64,512]{1,0:T(8,128)(2,1)}, bf16[64,512]{1,0:T(8,128)(2,1)S(1)}, u32[]{:S(2)}, u32[]{:S(2)}) collective-permute-start(bf16[64,512]{1,0:T(8,128)(2,1)} %bitcast.28), channel_id=1, source_target_pairs={{0,2},{1,3},{2,0},{3,1},{4,6},{5,7},{6,4},{7,5},{8,10},{9,11},{10,... | collective-permute-start | bytes 196616 | tf_op jit(solution)/shard_map/ppermute | solution.py:285
  3.8 25.5 %collective-permute-start = (bf16[512,512]{1,0:T(8,128)(2,1)}, bf16[512,512]{1,0:T(8,128)(2,1)S(1)}, u32[]{:S(2)}, u32[]{:S(2)}) collective-permute-start(bf16[512,512]{1,0:T(8,128)(2,1)} %refs_0_.7), channel_id=1, source_target_pairs={{0,1},{1,0},{2,3},{3,2},{4,5},{5,4},{6,7},{7,6},{8,9},{9,8},{10,11... | collective-permute-start | bytes 1572872 | tf_op jit(solution)/shard_map/ppermute | solution.py:285
  3.8 25.5 %collective-permute-start.3 = (bf16[64,512]{1,0:T(8,128)(2,1)}, bf16[64,512]{1,0:T(8,128)(2,1)S(1)}, u32[]{:S(2)}, u32[]{:S(2)}) collective-permute-start(bf16[64,512]{1,0:T(8,128)(2,1)} %bitcast.29), channel_id=1, source_target_pairs={{0,1},{1,0},{2,3},{3,2},{4,5},{5,4},{6,7},{7,6},{8,9},{9,8},{10,11... | collective-permute-start | bytes 196616 | tf_op jit(solution)/shard_map/ppermute | solution.py:285
  17.2 8.4 %copy-start.10 = (bf16[64,512]{1,0:T(8,128)(2,1)}, bf16[64,512]{1,0:T(8,128)(2,1)S(1)}, u32[]{:S(2)}) copy-start(bf16[64,512]{1,0:T(8,128)(2,1)S(1)} %collective-permute-done.4.refs_6_) | copy-start | bytes 196612
  17.2 12.0 %collective-permute-start.5 = (bf16[64,512]{1,0:T(8,128)(2,1)S(1)}, bf16[64,512]{1,0:T(8,128)(2,1)S(1)}, u32[]{:S(2)}, u32[]{:S(2)}) collective-permute-start(bf16[64,512]{1,0:T(8,128)(2,1)S(1)} %collective-permute-done.4.refs_6_), channel_id=1, source_target_pairs={{0,1},{1,0},{2,3},{3,2},{4,5},{5,4},{6,7},{7,6},{8,9},{9,8},{10,11... | collective-permute-start | bytes 196616 | tf_op jit(solution)/shard_map/ppermute | solution.py:285
  17.2 8.4 %copy-start.7 = (bf16[512,512]{1,0:T(8,128)(2,1)}, bf16[512,512]{1,0:T(8,128)(2,1)S(1)}, u32[]{:S(2)}) copy-start(bf16[512,512]{1,0:T(8,128)(2,1)S(1)} %collective-permute-done.1.refs_2_) | copy-start | bytes 1572868
  17.3 12.1 %collective-permute-start.2 = (bf16[512,512]{1,0:T(8,128)(2,1)S(1)}, bf16[512,512]{1,0:T(8,128)(2,1)S(1)}, u32[]{:S(2)}, u32[]{:S(2)}) collective-permute-start(bf16[512,512]{1,0:T(8,128)(2,1)S(1)} %collective-permute-done.1.refs_2_), channel_id=1, source_target_pairs={{0,1},{1,0},{2,3},{3,2},{4,5},{5,4},{6,7},{7,6},{8,9},{9,8},{10,11... | collective-permute-start | bytes 1572872 | tf_op jit(solution)/shard_map/ppermute | solution.py:285
  17.8 7.9 %copy-start.1 = (bf16[512,32,128]{2,1,0:T(8,128)(2,1)S(1)}, bf16[512,32,128]{2,1,0:T(8,128)(2,1)}, u32[]{:S(2)}) copy-start(bf16[512,32,128]{2,1,0:T(8,128)(2,1)} %param.9) | copy-start | bytes 12582916
  29.3 0.6 copy-start.11
  29.3 0.6 copy-start.12
  29.3 0.8 copy-start.8
  29.3 1.0 copy-start.9
  164.7 53.5 %copy-start.5 = (f32[8,512,128]{2,1,0:T(8,128)S(1)}, f32[8,512,128]{2,1,0:T(8,128)}, u32[]{:S(2)}) copy-start(f32[8,512,128]{2,1,0:T(8,128)} %get-tuple-element.60) | copy-start | bytes 6291460
  210.4 19.3 %collective-permute-start.6 = (f32[2,576,512]{2,1,0:T(8,128)}, f32[2,576,512]{2,1,0:T(8,128)S(1)}, u32[]{:S(2)}, u32[]{:S(2)}) collective-permute-start(f32[2,576,512]{2,1,0:T(8,128)} %get-tuple-element.53), channel_id=1, source_target_pairs={{0,1},{1,0},{2,3},{3,2},{4,5},{5,4},{6,7},{7,6},{8,9},{9,8},{10,11... | collective-permute-start | bytes 7077896 | tf_op jit(solution)/shard_map/ppermute | solution.py:285
  210.5 7.7 %collective-permute-start.23 = (f32[8,512,128]{2,1,0:T(8,128)}, f32[8,512,128]{2,1,0:T(8,128)S(1)}, u32[]{:S(2)}, u32[]{:S(2)}) collective-permute-start(f32[8,512,128]{2,1,0:T(8,128)} %get-tuple-element.61), channel_id=1, source_target_pairs={{0,1},{1,0},{2,3},{3,2},{4,5},{5,4},{6,7},{7,6},{8,9},{9,8},{10,11... | collective-permute-start | bytes 6291464 | tf_op jit(solution)/shard_map/ppermute | solution.py:285
  211.0 10.2 %collective-permute-start.14 = (f32[8,512,128]{2,1,0:T(8,128)}, f32[8,512,128]{2,1,0:T(8,128)S(1)}, u32[]{:S(2)}, u32[]{:S(2)}) collective-permute-start(f32[8,512,128]{2,1,0:T(8,128)} %get-tuple-element.55), channel_id=1, source_target_pairs={{0,1},{1,0},{2,3},{3,2},{4,5},{5,4},{6,7},{7,6},{8,9},{9,8},{10,11... | collective-permute-start | bytes 6291464 | tf_op jit(solution)/shard_map/ppermute | solution.py:285
  211.0 13.2 %collective-permute-start.17 = (f32[8,512,128]{2,1,0:T(8,128)}, f32[8,512,128]{2,1,0:T(8,128)S(1)}, u32[]{:S(2)}, u32[]{:S(2)}) collective-permute-start(f32[8,512,128]{2,1,0:T(8,128)} %get-tuple-element.57), channel_id=1, source_target_pairs={{0,1},{1,0},{2,3},{3,2},{4,5},{5,4},{6,7},{7,6},{8,9},{9,8},{10,11... | collective-permute-start | bytes 6291464 | tf_op jit(solution)/shard_map/ppermute | solution.py:285
  211.5 15.7 %collective-permute-start.20 = (f32[8,512,128]{2,1,0:T(8,128)}, f32[8,512,128]{2,1,0:T(8,128)S(1)}, u32[]{:S(2)}, u32[]{:S(2)}) collective-permute-start(f32[8,512,128]{2,1,0:T(8,128)} %get-tuple-element.59), channel_id=1, source_target_pairs={{0,1},{1,0},{2,3},{3,2},{4,5},{5,4},{6,7},{7,6},{8,9},{9,8},{10,11... | collective-permute-start | bytes 6291464 | tf_op jit(solution)/shard_map/ppermute | solution.py:285
  218.2 3.0 copy-start.6
  219.8 210.2 %collective-permute-start.24 = (f32[8,512,128]{2,1,0:T(8,128)}, f32[8,512,128]{2,1,0:T(8,128)}, u32[]{:S(2)}, u32[]{:S(2)}) collective-permute-start(f32[8,512,128]{2,1,0:T(8,128)} %add.54), channel_id=1, source_target_pairs={{0,2},{1,3},{2,0},{3,1},{4,6},{5,7},{6,4},{7,5},{8,10},{9,11},{10,... | collective-permute-start | bytes 6291464 | tf_op jit(solution)/shard_map/ppermute | solution.py:285
  221.2 3.0 copy-start.4
  222.7 215.1 %collective-permute-start.15 = (f32[8,512,128]{2,1,0:T(8,128)}, f32[8,512,128]{2,1,0:T(8,128)}, u32[]{:S(2)}, u32[]{:S(2)}) collective-permute-start(f32[8,512,128]{2,1,0:T(8,128)} %add.48), channel_id=1, source_target_pairs={{0,2},{1,3},{2,0},{3,1},{4,6},{5,7},{6,4},{7,5},{8,10},{9,11},{10,... | collective-permute-start | bytes 6291464 | tf_op jit(solution)/shard_map/ppermute | solution.py:285
  224.2 3.0 copy-start.3
  225.8 214.9 %collective-permute-start.18 = (f32[8,512,128]{2,1,0:T(8,128)}, f32[8,512,128]{2,1,0:T(8,128)}, u32[]{:S(2)}, u32[]{:S(2)}) collective-permute-start(f32[8,512,128]{2,1,0:T(8,128)} %add.50), channel_id=1, source_target_pairs={{0,2},{1,3},{2,0},{3,1},{4,6},{5,7},{6,4},{7,5},{8,10},{9,11},{10,... | collective-permute-start | bytes 6291464 | tf_op jit(solution)/shard_map/ppermute | solution.py:285
  227.2 2.5 copy-start.2
  228.7 205.3 %collective-permute-start.21 = (f32[8,512,128]{2,1,0:T(8,128)}, f32[8,512,128]{2,1,0:T(8,128)}, u32[]{:S(2)}, u32[]{:S(2)}) collective-permute-start(f32[8,512,128]{2,1,0:T(8,128)} %add.52), channel_id=1, source_target_pairs={{0,2},{1,3},{2,0},{3,1},{4,6},{5,7},{6,4},{7,5},{8,10},{9,11},{10,... | collective-permute-start | bytes 6291464 | tf_op jit(solution)/shard_map/ppermute | solution.py:285
  231.4 196.4 %collective-permute-start.7 = (f32[576,512]{1,0:T(8,128)}, f32[576,512]{1,0:T(8,128)S(1)}, u32[]{:S(2)}, u32[]{:S(2)}) collective-permute-start(f32[576,512]{1,0:T(8,128)} %slice_bitcast_fusion), channel_id=1, source_target_pairs={{0,2},{1,3},{2,0},{3,1},{4,6},{5,7},{6,4},{7,5},{8,10},{9,11},{10,... | collective-permute-start | bytes 3538952 | tf_op jit(solution)/shard_map/ppermute | solution.py:285
  428.2 17.2 %collective-permute-start.8 = (f32[288,256]{1,0:T(8,128)S(1)}, f32[288,256]{1,0:T(8,128)S(1)}, u32[]{:S(2)}, u32[]{:S(2)}) collective-permute-start(f32[288,256]{1,0:T(8,128)S(1)} %get-tuple-element.78), channel_id=1, source_target_pairs={{0,4},{4,0},{8,12},{12,8},{1,5},{5,1},{9,13},{13,9},{2,6},{6,2},{1... | collective-permute-start | bytes 884744 | tf_op jit(solution)/shard_map/ppermute | solution.py:285
  430.0 15.4 %collective-permute-start.11 = (f32[288,256]{1,0:T(8,128)S(1)}, f32[288,256]{1,0:T(8,128)S(1)}, u32[]{:S(2)}, u32[]{:S(2)}) collective-permute-start(f32[288,256]{1,0:T(8,128)S(1)} %get-tuple-element.79), channel_id=1, source_target_pairs={{0,4},{4,0},{8,12},{12,8},{1,5},{5,1},{9,13},{13,9},{2,6},{6,2},{1... | collective-permute-start | bytes 884744 | tf_op jit(solution)/shard_map/ppermute | solution.py:285
  434.0 62.5 %collective-permute-start.25 = (f32[8,512,128]{2,1,0:T(8,128)}, f32[8,512,128]{2,1,0:T(8,128)}, u32[]{:S(2)}, u32[]{:S(2)}) collective-permute-start(f32[8,512,128]{2,1,0:T(8,128)} %add.55.refs_0_), channel_id=1, source_target_pairs={{0,1},{1,0},{2,3},{3,2},{4,5},{5,4},{6,7},{7,6},{8,9},{9,8},{10,11... | collective-permute-start | bytes 6291464 | tf_op jit(solution)/shard_map/ppermute | solution.py:285
  437.8 64.4 %collective-permute-start.22 = (f32[8,512,128]{2,1,0:T(8,128)}, f32[8,512,128]{2,1,0:T(8,128)}, u32[]{:S(2)}, u32[]{:S(2)}) collective-permute-start(f32[8,512,128]{2,1,0:T(8,128)} %add.53.refs_0_), channel_id=1, source_target_pairs={{0,1},{1,0},{2,3},{3,2},{4,5},{5,4},{6,7},{7,6},{8,9},{9,8},{10,11... | collective-permute-start | bytes 6291464 | tf_op jit(solution)/shard_map/ppermute | solution.py:285
  440.7 4.7 copy-start
  440.8 72.8 %collective-permute-start.16 = (f32[8,512,128]{2,1,0:T(8,128)S(1)}, f32[8,512,128]{2,1,0:T(8,128)}, u32[]{:S(2)}, u32[]{:S(2)}) collective-permute-start(f32[8,512,128]{2,1,0:T(8,128)S(1)} %add.49.refs_0_), channel_id=1, source_target_pairs={{0,1},{1,0},{2,3},{3,2},{4,5},{5,4},{6,7},{7,6},{8,9},{9,8},{10,11... | collective-permute-start | bytes 6291464 | tf_op jit(solution)/shard_map/ppermute | solution.py:285
  445.4 62.5 %collective-permute-start.19 = (f32[8,512,128]{2,1,0:T(8,128)}, f32[8,512,128]{2,1,0:T(8,128)}, u32[]{:S(2)}, u32[]{:S(2)}) collective-permute-start(f32[8,512,128]{2,1,0:T(8,128)} %add.51.refs_0_), channel_id=1, source_target_pairs={{0,1},{1,0},{2,3},{3,2},{4,5},{5,4},{6,7},{7,6},{8,9},{9,8},{10,11... | collective-permute-start | bytes 6291464 | tf_op jit(solution)/shard_map/ppermute | solution.py:285
  445.5 16.9 %collective-permute-start.12 = (f32[288,256]{1,0:T(8,128)S(1)}, f32[288,256]{1,0:T(8,128)S(1)}, u32[]{:S(2)}, u32[]{:S(2)}) collective-permute-start(f32[288,256]{1,0:T(8,128)S(1)} %get-tuple-element.77), channel_id=1, source_target_pairs={{0,8},{4,12},{8,0},{12,4},{1,9},{5,13},{9,1},{13,5},{2,10},{6,14},... | collective-permute-start | bytes 884744 | tf_op jit(solution)/shard_map/ppermute | solution.py:285
  462.4 15.9 %collective-permute-start.9 = (f32[288,256]{1,0:T(8,128)S(1)}, f32[288,256]{1,0:T(8,128)S(1)}, u32[]{:S(2)}, u32[]{:S(2)}) collective-permute-start(f32[288,256]{1,0:T(8,128)S(1)} %get-tuple-element.76), channel_id=1, source_target_pairs={{0,8},{4,12},{8,0},{12,4},{1,9},{5,13},{9,1},{13,5},{2,10},{6,14},... | collective-permute-start | bytes 884744 | tf_op jit(solution)/shard_map/ppermute | solution.py:285
  478.3 7.9 %collective-permute-start.13 = (f32[288,256]{1,0:T(8,128)S(1)}, f32[288,256]{1,0:T(8,128)S(1)}, u32[]{:S(2)}, u32[]{:S(2)}) collective-permute-start(f32[288,256]{1,0:T(8,128)S(1)} %add.47), channel_id=1, source_target_pairs={{0,4},{4,0},{8,12},{12,8},{1,5},{5,1},{9,13},{13,9},{2,6},{6,2},{1... | collective-permute-start | bytes 884744 | tf_op jit(solution)/shard_map/ppermute | solution.py:285
  486.2 8.4 %collective-permute-start.10 = (f32[288,256]{1,0:T(8,128)S(1)}, f32[288,256]{1,0:T(8,128)S(1)}, u32[]{:S(2)}, u32[]{:S(2)}) collective-permute-start(f32[288,256]{1,0:T(8,128)S(1)} %add.45), channel_id=1, source_target_pairs={{0,4},{4,0},{8,12},{12,8},{1,5},{5,1},{9,13},{13,9},{2,6},{6,2},{1... | collective-permute-start | bytes 884744 | tf_op jit(solution)/shard_map/ppermute | solution.py:285

commit v2 on v1

v2 whole, which is shorter than its diff:
```python
import functools
import jax
import jax.numpy as jnp
from jax import lax
from jax.experimental import pallas as pl
from jax.experimental.pallas import tpu as pltpu
from jax.sharding import PartitionSpec as P

NEG_BIG = -1.0e30
LOG2E = 1.4426950408889634
F32 = jnp.float32
BF16 = jnp.bfloat16
Y_HEADS = 24


def mm(a, b):
    return jnp.dot(a, b, preferred_element_type=F32)


def mm_nt(a, b):
    return lax.dot_general(a, b, (((1,), (1,)), ((), ())), preferred_element_type=F32)


def attn_body(n_cp, half, scale, n_h, n_y, *refs):
    n_blk = n_cp
    c_refs, rt_refs = refs[:n_blk], refs[n_blk:2 * n_blk]
    qt_ref, do_ref, wk_ref, wv_ref, wk_old, wv_old = refs[2 * n_blk:2 * n_blk + 6]
    rest = refs[2 * n_blk + 6:]
    (ot_ref, dqt_ref, acc0, acc1, acc2, acc3, done_ref, part_ref,
     ct, kk, kt, v_s, vt_s, p_s, dkv, dr_s, o_s, dq_s, q_s, qt_s, dot_s, bias, dw_s,
     snd, own, chip, far, d_send, d_recv, y_send, y_recv, out_sem) = rest
    h = pl.program_id(0)
    me = lax.axis_index('cp')
    d_nope = do_ref.shape[2]
    d_qk = qt_ref.shape[1]
    d_rope = d_qk - d_nope
    blk, _ = c_refs[0].shape
    keys = blk * n_blk
    n_t = 2 * n_cp + 1
    c2 = scale * LOG2E
    acc_refs = [acc0, acc1, acc2, acc3]
    even = lax.rem(me, 2) == 0
    mate = me + 1 - 2 * lax.rem(me, 2)
    across = lax.rem(me + 2, n_cp)

    def to_mate(g, slot):
        return pltpu.make_async_remote_copy(
            src_ref=snd.at[slot], dst_ref=chip.at[g], send_sem=d_send.at[slot], recv_sem=d_recv.at[g],
            device_id={'cp': mate}, device_id_type=pl.DeviceIdType.MESH)

    def to_across(g):
        return pltpu.make_async_remote_copy(
            src_ref=chip.at[g], dst_ref=far.at[g], send_sem=y_send.at[g], recv_sem=y_recv.at[g],
            device_id={'cp': across}, device_id_type=pl.DeviceIdType.MESH)

    def to_part(g):
        return pltpu.make_async_copy(chip.at[g], part_ref.at[g - n_y], out_sem.at[g])

    def to_done(g):
        return pltpu.make_async_copy(far.at[g], done_ref.at[g], out_sem.at[g])

    def merge(g, slot):
        to_mate(g, slot).wait()
        chip[g] += own[slot]

        @pl.when(g < n_y)
        def _():
            to_across(g).start()

        @pl.when(g >= n_y)
        def _():
            to_part(g).start()

    @pl.when(h == 0)
    def _():
        barrier = pltpu.get_barrier_semaphore()
        for peer in (mate, across):
            pl.semaphore_signal(barrier, inc=1, device_id={'cp': peer}, device_id_type=pl.DeviceIdType.MESH)
        pl.semaphore_wait(barrier, 2)
        for j in range(n_blk):
            rows = slice(j * blk, (j + 1) * blk)
            ct[:, rows] = c_refs[j][...].T
            rt = rt_refs[j][...]
            kt[d_nope:, rows] = rt
            kk[rows, d_nope:] = jnp.concatenate([rt, jnp.zeros((128 - d_rope, blk), BF16)], axis=0).T
        qt_s[d_qk:, :] = jnp.zeros((qt_s.shape[0] - d_qk, qt_s.shape[1]), BF16)
        dr_s[...] = jnp.zeros_like(dr_s)
        dkv[...] = jnp.zeros_like(dkv)
        k_io = lax.broadcasted_iota(jnp.int32, (half, half), 0)
        q_io = lax.broadcasted_iota(jnp.int32, (half, half), 1)
        bias[0] = jnp.zeros((half, half), F32)
        bias[1] = jnp.where(k_io <= q_io, 0.0, NEG_BIG)
        for ref in acc_refs:
            ref[...] = jnp.zeros_like(ref)

    def post(j, w):
        rows = slice(j * half, (j + 1) * half)
        g = dkv[rows, :].astype(BF16)
        ref = acc_refs[j // 2]
        part = mm(ct[:, rows], g)
        dw_s[...] = part if j == 0 else dw_s[...] + part
        o = j % 2 * half
        ref[o:o + half, :] += mm_nt(g, w)
        dkv[rows, :] = jnp.zeros((half, dkv.shape[1]), F32)

    def post_out():
        slot = lax.rem(h + 1, 2)
        dwk, dwv = dw_s[:, :d_nope], dw_s[:, d_nope:]
        own[slot] = jnp.where(even, dwk, dwv)
        snd[slot] = jnp.where(even, dwv, dwk)

    @pl.when(h < n_h)
    def _():
        w = jnp.concatenate([wk_ref[0], wv_ref[0]], axis=1)
        w_old = jnp.concatenate([wk_old[0], wv_old[0]], axis=1)
        for j in range(0, keys, half):
            rows = slice(j, j + half)
            kv = mm(c_refs[j // blk][j % blk:j % blk + half, :], w).astype(BF16)
            kk[rows, :d_nope] = kv[:, :d_nope]
            v_s[rows, :] = kv[:, d_nope:]
            kt[:d_nope, rows] = kv[:, :d_nope].T
            vt_s[:, rows] = kv[:, d_nope:].T
        qt_s[:d_qk, :] = qt_ref[0]
        q_s[...] = qt_s[...].T
        dot_s[...] = do_ref[0].T

        tiles = []
        for t in range(n_t):
            if t == 0:
                is_a, qo, kp = True, 0, me * 0
            elif t < n_cp:
                is_a = t <= me
                qo = pl.multiple_of(jnp.where(is_a, 0, half), half)
                kp = jnp.where(is_a, t, t - me - 1)
            else:
                is_a, qo, kp = None, half, t - me - 1
            low = kp < n_cp
            owner = jnp.where(low, kp, 2 * n_cp - 1 - kp)
            e0, e1 = lax.rem(owner, 2) + lax.rem(me, 2), lax.div(owner, 2) + lax.div(me, 2)
            slot = lax.rem(e0, 2) + 2 * lax.rem(e1, 2)
            ko = pl.multiple_of(slot * blk + jnp.where(low, 0, half), half)
            tiles.append((t, is_a, qo, ko))

        def pick(is_a, a, b):
            return b if is_a is None else a if is_a is True else jnp.where(is_a, a, b)

        def put(is_a, cur, new):
            a, b = cur
            if is_a is True:
                return (new, b)
            if is_a is None:
                return (a, new)
            return (jnp.where(is_a, new, a), jnp.where(is_a, b, new))

        neg = jnp.full((1, half), NEG_BIG, F32)
        zero = jnp.zeros((1, half), F32)
        m, l = (neg, neg), (zero, zero)
        for t, is_a, qo, ko in tiles:
            s = mm(kk[pl.ds(ko, half), :], qt_s[:, pl.ds(qo, half)])
            if t == n_t - 1:
                s = s + bias[1]
            elif t < n_cp:
                s = s + bias[jnp.where(t == me, 1, 0)]
            p_s[t] = s
            m = put(is_a, m, jnp.maximum(pick(is_a, *m), jnp.max(s, axis=0, keepdims=True)))
        m = tuple(x * c2 for x in m)
        acc_o = None
        for t, is_a, qo, ko in tiles:
            p = jnp.exp2(p_s[t] * c2 - pick(is_a, *m))
            l = put(is_a, l, pick(is_a, *l) + jnp.sum(p, axis=0, keepdims=True))
            p_s[t] = p
            o = mm(vt_s[:, pl.ds(ko, half)], p.astype(BF16))
            if t == 0:
                o_s[:, :half] = o
                o_s[:, half:] = jnp.zeros_like(o)
            elif t < n_cp:
                o_s[:, pl.ds(qo, half)] += o
            else:
                acc_o = o if acc_o is None else acc_o + o
            if t < 2 * n_blk:
                post(t, w_old)
        o_s[:, half:] += acc_o
        post_out()
        linv = tuple(1.0 / x for x in l)
        dd = []
        for i in range(2):
            cols = slice(i * half, (i + 1) * half)
            o = o_s[:, cols] * linv[i]
            ot_ref[0, :, cols] = o.astype(BF16)
            dd.append(jnp.sum(o * dot_s[:, cols].astype(F32), axis=0, keepdims=True))

        acc_q = None
        for t, is_a, qo, ko in tiles:
            p = p_s[t] * (pick(is_a, *linv))
            rows = pl.ds(ko, half)
            dp = mm(v_s[rows, :], dot_s[:, pl.ds(qo, half)])
            ds = (p * (dp - pick(is_a, *dd))).astype(BF16)
            dv = mm(p.astype(BF16), do_ref[0, pl.ds(qo, half), :])
            dk = mm(ds, q_s[pl.ds(qo, half), :]) * scale
            dq = mm(kt[:, rows], ds)
            dkv[rows, :d_nope] += dk[:, :d_nope]
            dkv[rows, d_nope:] += dv
            dr_s[rows, :] += dk[:, d_nope:]
            if t == 0:
                dq_s[:, :half] = dq
                dq_s[:, half:] = jnp.zeros_like(dq)
            elif t < n_cp:
                dq_s[:, pl.ds(qo, half)] += dq
            else:
                acc_q = dq if acc_q is None else acc_q + dq
        dqt_ref[0, :, :half] = dq_s[:, :half]
        dqt_ref[0, :, half:] = dq_s[:, half:] + acc_q

        @pl.when(h >= 2)
        def _():
            merge(h - 2, lax.rem(h, 2))

        @pl.when(h >= 1)
        def _():
            to_mate(h - 1, lax.rem(h + 1, 2)).start()

    @pl.when(h == n_h)
    def _():
        w_old = jnp.concatenate([wk_old[0], wv_old[0]], axis=1)
        for j in range(2 * n_blk):
            post(j, w_old)
        for j in range(n_blk):
            acc_refs[j][blk:, :] = dr_s[j * blk:(j + 1) * blk, :].T[:d_rope, :]
        post_out()
        to_mate(n_h - 1, (n_h - 1) % 2).start()
        merge(n_h - 2, n_h % 2)
        merge(n_h - 1, (n_h - 1) % 2)

        def finish(g, carry):
            to_across(g).wait()
            far[g] += chip[g]
            to_done(g).start()
            return carry

        lax.fori_loop(0, n_y, finish, 0)

        def drain(g, carry):
            to_done(g).wait()
            return carry

        lax.fori_loop(0, n_y, drain, 0)
        for g in range(n_y, n_h):
            to_part(g).wait()


def attn_call(n_cp, scale, n_y, cs, rts, qt, do_h, wk_h, wv_h):
    n_h, d_qk, rows = qt.shape
    blk, rank = cs[0].shape
    d_rope = rts[0].shape[0]
    keys = blk * n_cp
    d_val = do_h.shape[2]
    half = rows // 2
    n_t = 2 * n_cp + 1
    full = lambda *shape: pl.BlockSpec(shape, lambda h: (0,) * len(shape))
    head = lambda *shape: pl.BlockSpec((1,) + shape, lambda h: (jnp.minimum(h, n_h - 1),) + (0,) * len(shape))
    prev = lambda *shape: pl.BlockSpec((1,) + shape, lambda h: (jnp.maximum(h - 1, 0),) + (0,) * len(shape))
    anyspec = pl.BlockSpec(memory_space=pl.ANY)
    in_specs = [full(blk, rank)] * n_cp + [full(d_rope, blk)] * n_cp + [
        head(d_qk, rows), head(rows, d_val), head(rank, d_val), head(rank, d_val),
        prev(rank, d_val), prev(rank, d_val)]
    args = [*cs, *rts, qt, do_h, wk_h, wv_h, wk_h, wv_h]
    acc = (blk + d_rope, rank)
    out_shape = [jax.ShapeDtypeStruct((n_h, d_val, rows), BF16),
                 jax.ShapeDtypeStruct((n_h, d_qk, rows), F32),
                 *[jax.ShapeDtypeStruct(acc, F32)] * n_cp,
                 jax.ShapeDtypeStruct((n_y, rank, d_val), F32),
                 jax.ShapeDtypeStruct((n_h - n_y, rank, d_val), F32)]
    out_specs = [head(d_val, rows), head(d_qk, rows), *[full(*acc)] * n_cp, anyspec, anyspec]
    scratch = [pltpu.VMEM((rank, keys), BF16),
               pltpu.VMEM((keys, 256), BF16), pltpu.VMEM((d_qk, keys), BF16),
               pltpu.VMEM((keys, d_val), BF16), pltpu.VMEM((d_val, keys), BF16),
               pltpu.VMEM((n_t, half, half), F32),
               pltpu.VMEM((keys, 2 * d_val), F32), pltpu.VMEM((keys, 128), F32),
               pltpu.VMEM((d_val, rows), F32), pltpu.VMEM((d_qk, rows), F32),
               pltpu.VMEM((rows, 256), BF16), pltpu.VMEM((256, rows), BF16),
               pltpu.VMEM((d_val, rows), BF16), pltpu.VMEM((2, half, half), F32), pltpu.VMEM((rank, 2 * d_val), F32),
               pltpu.VMEM((2, rank, d_val), F32), pltpu.VMEM((2, rank, d_val), F32),
               pltpu.VMEM((n_h, rank, d_val), F32), pltpu.VMEM((n_y, rank, d_val), F32),
               pltpu.SemaphoreType.DMA((2,)), pltpu.SemaphoreType.DMA((n_h,)),
               pltpu.SemaphoreType.DMA((n_y,)), pltpu.SemaphoreType.DMA((n_y,)),
               pltpu.SemaphoreType.DMA((n_h,))]
    flops = n_h * (3 * 2 * keys * rank * 2 * d_val + n_t * half * half * 2 * 1024)
    return pl.pallas_call(
        functools.partial(attn_body, n_cp, half, scale, n_h, n_y),
        grid=(n_h + 1,), in_specs=in_specs, out_specs=out_specs, out_shape=out_shape,
        scratch_shapes=scratch,
        compiler_params=pltpu.CompilerParams(dimension_semantics=("arbitrary",), vmem_limit_bytes=63 * 2**20,
                                             collective_id=0, has_side_effects=True),
        cost_estimate=pl.CostEstimate(flops=flops, bytes_accessed=n_h * 2**20, transcendentals=0),
        name="attn",
    )(*args)


def place_body(mine, other, *refs):
    k_ref, v_ref = refs[-2:]
    even = lax.rem(lax.axis_index('cp'), 2) == 0
    for j in range(mine.shape[0]):
        a, b = mine[j], other[j]
        k_ref[:, j, :] = jnp.where(even, a, b)
        v_ref[:, j, :] = jnp.where(even, b, a)


def place(group, heads, mine, other, carry):
    n_g = 8
    n_h, rank, d_val = mine.shape
    step = 128
    ins = [pl.BlockSpec((n_g, step, d_val), lambda g, r: (g, r, 0))] * 2
    args = [mine, other]
    aliases = {}
    if carry is not None:
        aliases = {2: 0, 3: 1}
        args += list(carry)
        ins = ins + [pl.BlockSpec(memory_space=pl.ANY)] * 2
    out = jax.ShapeDtypeStruct((rank, heads, d_val), F32)
    return pl.pallas_call(
        place_body, grid=(n_h // n_g, rank // step), in_specs=ins,
        out_specs=[pl.BlockSpec((step, n_g, d_val), lambda g, r: (r, g + group, 0))] * 2,
        out_shape=[out, out], input_output_aliases=aliases,
        compiler_params=pltpu.CompilerParams(dimension_semantics=("arbitrary", "arbitrary")),
        cost_estimate=pl.CostEstimate(flops=n_h * 10 ** 8, bytes_accessed=4 * n_h * rank * d_val * 4, transcendentals=0),
        name="place",
    )(*args)


def rows_body(x_ref, o_ref, s_ref):
    for j in range(x_ref.shape[0]):
        s_ref[:, j, :] = x_ref[j].T.astype(F32)
    o_ref[...] = s_ref[...].astype(BF16)


def to_rows(x):
    n_g = 8
    heads, d_val, rows = x.shape
    return pl.pallas_call(
        rows_body, grid=(heads // n_g,),
        in_specs=[pl.BlockSpec((n_g, d_val, rows), lambda g: (g, 0, 0))],
        out_specs=pl.BlockSpec((rows, n_g, d_val), lambda g: (0, g, 0)),
        out_shape=jax.ShapeDtypeStruct((rows, heads, d_val), BF16),
        scratch_shapes=[pltpu.VMEM((rows, n_g, d_val), F32)],
        compiler_params=pltpu.CompilerParams(dimension_semantics=("arbitrary",)),
        cost_estimate=pl.CostEstimate(flops=10 ** 9, bytes_accessed=4 * heads * d_val * rows, transcendentals=0),
        name="to_rows",
    )(x)


def swap(x, axis, size, bit):
    return lax.ppermute(x, axis, [(i, i ^ bit) for i in range(size)])


def solution(mesh):
    n_cp = mesh.shape['cp']
    seq_spec = P(('dp', 'cp'), None)
    head_spec = P(('dp', 'cp'), 'tp', None)
    weight_spec = P(None, 'tp', None)
    grad_spec = P('dp', 'tp', None)

    def device_body(c_latent, k_rope, q_heads, d_out, w_uk, w_uv):
        rows = c_latent.shape[0]
        scale = q_heads.shape[2] ** -0.5
        heads = q_heads.shape[1]
        n_tp = mesh.shape['tp']
        rt = k_rope.T
        c2, r2 = swap(c_latent, 'cp', n_cp, 2), swap(rt, 'cp', n_cp, 2)
        c1, r1 = swap(c_latent, 'cp', n_cp, 1), swap(rt, 'cp', n_cp, 1)
        qt = jnp.transpose(q_heads, (1, 2, 0))
        do_h = jnp.transpose(d_out, (1, 0, 2))
        wk_h = jnp.transpose(w_uk, (1, 0, 2))
        wv_h = jnp.transpose(w_uv, (1, 0, 2))
        c2, r2, do_h, wk_h, wv_h = lax.optimization_barrier((c2, r2, do_h, wk_h, wv_h))
        c3, r3 = swap(c2, 'cp', n_cp, 1), swap(r2, 'cp', n_cp, 1)
        cs, rts = (c_latent, c1, c2, c3), (rt, r1, r2, r3)
        ot, dqt, a0, a1, a2, a3, done, part = attn_call(n_cp, scale, Y_HEADS, cs, rts, qt, do_h, wk_h, wv_h)
        g2 = swap(a3, 'cp', n_cp, 1)
        g0 = swap(a1, 'cp', n_cp, 1)
        dq = jnp.transpose(dqt * scale, (2, 0, 1))
        out = to_rows(ot)
        other = swap(done, 'cp', n_cp, 1)
        placed = place(0, heads, done, other, None)
        odd = lax.rem(lax.axis_index('tp'), 2) == 1
        n_col = a0.shape[1] // 2
        mid = a0.shape[0] // 2
        col = lambda v, i: v[:, i * n_col:(i + 1) * n_col]
        far = []
        for i in range(2):
            far.append(swap(col(a2, i) + col(g2, i), 'cp', n_cp, 2))

        def first_swap(x):
            lo, hi = x[:mid], x[mid:]
            y = swap(jnp.where(odd, lo, hi), 'tp', n_tp, 1)
            return jnp.where(odd, hi, lo) + y

        def last_swaps(x):
            y = swap(x, 'tp', n_tp, 2)
            x = x + y
            y = swap(x, 'tp', n_tp, 1)
            return jnp.concatenate([jnp.where(odd, y, x), jnp.where(odd, x, y)], axis=0)

        x0 = first_swap(col(a0, 0) + col(g0, 0) + far[0])
        x0, far1 = lax.optimization_barrier((x0, far[1]))
        x1 = first_swap(col(a0, 1) + col(g0, 1) + far1)
        halves = [last_swaps(x0), last_swaps(x1)]
        acc = jnp.concatenate(halves, axis=1)
        far = swap(part, 'cp', n_cp, 2)
        far, acc = lax.optimization_barrier((far, acc))
        total = part + far
        placed = place(Y_HEADS // 8, heads, total, swap(total, 'cp', n_cp, 1), placed)
        return (out, dq, acc[:rows], acc[rows:].T, placed[0], placed[1])

    return jax.shard_map(device_body, mesh=mesh,
                         in_specs=(seq_spec, seq_spec, head_spec, head_spec, weight_spec, weight_spec),
                         out_specs=(head_spec, head_spec, seq_spec, seq_spec, grad_spec, grad_spec),
                         check_vma=False)
```

time: 528 us -> 306 us (0.58); the launches traced: 520 us -> 305 us
  waiting for transfers between devices: 254 us -> 66.5 us
  Pallas kernels: 203 us -> 191 us
  local copies, waits for them, and re-layouts: 22.7 us -> 14.1 us
  other arithmetic: 22.8 us -> 17.5 us
    ppermute x26 -> x19, waiting for transfers between devices: 254 us -> 66.5 us  [swap(): return lax.ppermute(x, axis, [(i, i ^ bit) for i in range(size)])]
    add x13 -> x8, other arithmetic: 21.8 us -> 5.4 us  [the longest x1 2.4 us: device_body(): far.append(swap(col(a2, i) + col(g2, i), 'cp', n_cp, 2))]
    pallas_call x8 -> x4, Pallas kernels: 203 us -> 191 us  [the longest x1 162 us: attn_call(): pl.pallas_call(functools.partial(attn_body, n_cp, half, scale, n_h, n_y),...]
    transpose x1, other arithmetic: 0.66 us -> 11.8 us  [device_body(): dq = jnp.transpose(dqt * scale, (2, 0, 1))]
    unnamed x28 -> x25, local copies, waits for them, and re-layouts: 12.7 us -> 4.59 us
    ppermute x26 -> x19, starting transfers between devices: 16.1 us -> 14.8 us  [swap(): return lax.ppermute(x, axis, [(i, i ^ bit) for i in range(size)])]
  transfers between devices with their start and end apart: 26 -> 19, of which waited for: 9 -> 14; matrix products, arithmetic and copies ran while one was open for 9% -> 10% of each run, Pallas kernels for 3% -> 8%
where the time goes in v2:
time: 306 us; the launch traced here: 305 us
  Pallas kernels  191 us (62%)
  waiting for transfers between devices  66.5 us (22%)
  other arithmetic  17.5 us (6%)
  starting transfers between devices  14.8 us (5%)
  local copies, waits for them, and re-layouts  14.1 us (5%)
    pallas_call x1, Pallas kernels, attn_call(): pl.pallas_call(functools.partial(attn_body, n_cp, half, scale, n_h, n_y),...  162 us
    ppermute x19, waiting for transfers between devices, swap(): return lax.ppermute(x, axis, [(i, i ^ bit) for i in range(size)])  66.5 us
    pallas_call x2, Pallas kernels, place(): pl.pallas_call(place_body, grid=(n_h // n_g, rank // step), in_specs=ins,...  20.5 us
    ppermute x19, starting transfers between devices, swap(): return lax.ppermute(x, axis, [(i, i ^ bit) for i in range(size)])  14.8 us
    transpose x1, other arithmetic, device_body(): dq = jnp.transpose(dqt * scale, (2, 0, 1))  11.8 us
    pallas_call x1, Pallas kernels, to_rows(): pl.pallas_call(rows_body, grid=(heads // n_g,), in_specs=[pl.BlockSpec((n...  8.55 us
    transpose x1, local copies, waits for them, and re-layouts, device_body(): wv_h = jnp.transpose(w_uv, (1, 0, 2))  7.85 us
  transfers between devices with their start and end apart: 19, of which 14 were waited for; matrix products, arithmetic and copies ran while one was open for 10% of the time, Pallas kernels for 8%

profile of v2, /device:TPU:0, one launch (start us, length us, event | category | flops | bytes accessed | tf_op | source)
XLA Modules:
  0.0 305.3 jit_solution(16445423080680466535)
XLA Ops:
  0.6 0.6 collective-permute-start
  1.2 2.6 collective-permute-start.1
  3.8 0.1 collective-permute-start.2
  3.9 7.9 %copy_bitcast_fusion = (bf16[32,512,128]{2,1,0:T(8,128)(2,1)}, bf16[32,512,128]{2,1,0:T(8,128)(2,1)}) fusion(bf16[512,32,128]{2,1,0:T(8,128)(2,1)} %param.11, bf16[512,32,128]{2,1,0:T(8,128)(2,1)} %param.10), kind=kLoop, calls=%fused_computation.1 | loop fusion | bytes 16777216 | tf_op jit(solution)/shard_map/transpose | solution.py:373
  11.7 3.6 %copy.20 = bf16[512,32,128]{2,0,1:T(8,128)(2,1)} copy(bf16[512,32,128]{2,1,0:T(8,128)(2,1)S(1)} %copy-done.1) | data formatting | bytes 8388608 | tf_op args[3]
  15.4 2.6 collective-permute-done.2.refs_6_
  17.9 0.1 collective-permute-start.3
  18.0 0.5 collective-permute-start.4
  18.5 0.1 collective-permute-start.5
  18.6 1.4 collective-permute-done.4.refs_5_
  20.0 0.1 collective-permute-done.5.refs_7_
  20.1 0.9 copy-done.7
  21.0 162.4 %attn.1 = (bf16[32,128,512]{2,1,0:T(8,128)(2,1)}, f32[32,192,512]{2,1,0:T(8,128)}, f32[576,512]{1,0:T(8,128)}, f32[576,512]{1,0:T(8,128)}, f32[576,512]{1,0:T(8,...) custom-call(bf16[512,512]{1,0:T(8,128)(2,1)} %refs_0_.1, bf16[512,512]{1,0:T(8,128)(2,1)} %copy-done.5, ...), custom_call_target="tpu_custom_call" | custom-call | flops 90194313216 | bytes 33554432 | tf_op jit(solution)/shard_map/attn/pallas_call | solution.py:288
  183.4 0.4 collective-permute-start.8
  183.8 0.1 collective-permute-start.18
  184.0 0.4 collective-permute-start.7
  184.4 2.2 collective-permute-done.8
  186.5 2.4 slice_add_fusion.1
  188.9 2.0 collective-permute-start.11
  191.0 6.4 %collective-permute-done.7 = f32[576,512]{1,0:T(8,128)} collective-permute-done((f32[576,512]{1,0:T(8,128)}, f32[576,512]{1,0:T(8,128)}, u32[]{:S(2)}, u32[]{:S(2)}) %collective-permute-start.7) | collective-permute-done | bytes 1179680 | tf_op jit(solution)/shard_map/ppermute | solution.py:352
  197.3 8.1 %collective-permute-done.9 = f32[576,256]{1,0:T(8,128)} collective-permute-done((f32[576,256]{1,0:T(8,128)}, f32[576,256]{1,0:T(8,128)}, u32[]{:S(2)}, u32[]{:S(2)}) %collective-permute-start.9) | collective-permute-done | bytes 589856 | tf_op jit(solution)/shard_map/ppermute | solution.py:352
  205.5 1.4 fusion.1
  206.9 1.6 collective-permute-start.10
  208.5 0.2 collective-permute-start.6
  208.7 6.1 %collective-permute-done.10 = f32[288,256]{1,0:T(8,128)S(1)} collective-permute-done((f32[288,256]{1,0:T(8,128)S(1)}, f32[288,256]{1,0:T(8,128)S(1)}, u32[]{:S(2)}, u32[]{:S(2)}) %collective-permute-start.10) | collective-permute-done | bytes 294944 | tf_op jit(solution)/shard_map/ppermute | solution.py:352
  214.8 0.1 select_add_fusion.1
  214.8 3.1 %collective-permute-done.11 = f32[576,256]{1,0:T(8,128)S(1)} collective-permute-done((f32[576,256]{1,0:T(8,128)}, f32[576,256]{1,0:T(8,128)S(1)}, u32[]{:S(2)}, u32[]{:S(2)}) %collective-permute-start.11) | collective-permute-done | bytes 589856 | tf_op jit(solution)/shard_map/ppermute | solution.py:352
  218.0 1.2 fusion
  219.2 1.6 collective-permute-start.14
  220.9 2.6 collective-permute-start.12
  223.5 9.9 %collective-permute-done.14 = f32[288,256]{1,0:T(8,128)S(1)} collective-permute-done((f32[288,256]{1,0:T(8,128)S(1)}, f32[288,256]{1,0:T(8,128)S(1)}, u32[]{:S(2)}, u32[]{:S(2)}) %collective-permute-start.14) | collective-permute-done | bytes 294944 | tf_op jit(solution)/shard_map/ppermute | solution.py:352
  233.4 0.6 collective-permute-start.15
  234.0 6.4 %collective-permute-done.12 = f32[288,256]{1,0:T(8,128)S(1)} collective-permute-done((f32[288,256]{1,0:T(8,128)S(1)}, f32[288,256]{1,0:T(8,128)S(1)}, u32[]{:S(2)}, u32[]{:S(2)}) %collective-permute-start.12) | collective-permute-done | bytes 294944 | tf_op jit(solution)/shard_map/ppermute | solution.py:352
  240.5 1.2 collective-permute-start.13
  241.7 6.8 %collective-permute-done.15 = f32[288,256]{1,0:T(8,128)S(1)} collective-permute-done((f32[288,256]{1,0:T(8,128)S(1)}, f32[288,256]{1,0:T(8,128)S(1)}, u32[]{:S(2)}, u32[]{:S(2)}) %collective-permute-start.15) | collective-permute-done | bytes 294944 | tf_op jit(solution)/shard_map/ppermute | solution.py:352
  248.5 0.1 collective-permute-start.16
  248.6 3.3 %collective-permute-done.13 = f32[288,256]{1,0:T(8,128)S(1)} collective-permute-done((f32[288,256]{1,0:T(8,128)S(1)}, f32[288,256]{1,0:T(8,128)S(1)}, u32[]{:S(2)}, u32[]{:S(2)}) %collective-permute-start.13) | collective-permute-done | bytes 294944 | tf_op jit(solution)/shard_map/ppermute | solution.py:352
  252.0 5.9 %collective-permute-done.16 = f32[288,256]{1,0:T(8,128)S(1)} collective-permute-done((f32[288,256]{1,0:T(8,128)S(1)}, f32[288,256]{1,0:T(8,128)S(1)}, u32[]{:S(2)}, u32[]{:S(2)}) %collective-permute-start.16) | collective-permute-done | bytes 294944 | tf_op jit(solution)/shard_map/ppermute | solution.py:352
  257.9 0.1 maximum_maximum_fusion
  258.0 4.3 %collective-permute-done.6 = f32[8,512,128]{2,1,0:T(8,128)S(1)} collective-permute-done((f32[8,512,128]{2,1,0:T(8,128)S(1)}, f32[8,512,128]{2,1,0:T(8,128)S(1)}, u32[]{:S(2)}, u32[]{:S(2)}) %collective-permute-start.6) | collective-permute-done | bytes 2097184 | tf_op jit(solution)/shard_map/ppermute | solution.py:352
  262.3 0.2 add.43.mine
  262.6 0.1 collective-permute-start.17
  262.6 8.5 %to_rows.1 = bf16[512,32,128]{2,1,0:T(8,128)(2,1)} custom-call(bf16[32,128,512]{2,1,0:T(8,128)(2,1)} %get-tuple-element.32.x_ref), custom_call_target="tpu_custom_call" | custom-call | flops 1000000000 | bytes 8388608 | tf_op jit(solution)/shard_map/to_rows/pallas_call | solution.py:339
  271.2 11.8 %multiply_bitcast_fusion = f32[512,32,192]{0,2,1:T(8,128)} fusion(f32[32,192,512]{2,1,0:T(8,128)} %get-tuple-element.33), kind=kLoop, calls=%fused_computation | loop fusion | flops 3145728 | bytes 25165824 | tf_op jit(solution)/shard_map/transpose | solution.py:380
  283.0 1.0 slice.54
  284.1 0.7 slice_bitcast_fusion
  284.7 14.9 %place.2 = (f32[512,32,128]{2,1,0:T(8,128)}, f32[512,32,128]{2,1,0:T(8,128)}) custom-call(f32[24,512,128]{2,1,0:T(8,128)} %get-tuple-element.43.mine, f32[24,512,128]{2,1,0:T(8,128)} %collective-permute-done.18.other), custom_call_target="tpu_custom_call" | custom-call | flops 2400000000 | bytes 25165824 | tf_op jit(solution)/shard_map/place/pallas_call | solution.py:320
  299.6 5.7 %place.3 = (f32[512,32,128]{2,1,0:T(8,128)}, f32[512,32,128]{2,1,0:T(8,128)}) custom-call(f32[8,512,128]{2,1,0:T(8,128)} %copy-done, f32[8,512,128]{2,1,0:T(8,128)} %collective-permute-done.17.other, f32[512,32,128]{2,1,0:T(8,128)} %get-tuple-element.44.refs_0_, f32[512,32,128]{2,1,0:T(8,128)} %get-tuple-element.45.refs_1_), custom_call_target="tpu_custom_call", output_to_operand_aliasing={{0}: (2, {}), {1}: (3, {})} | custom-call | flops 800000000 | bytes 8388608 | tf_op jit(solution)/shard_map/place/pallas_call | solution.py:320
  (36 shorter events, 0.4 us)
Async XLA Ops:
  0.6 19.3 %collective-permute-start = (bf16[512,512]{1,0:T(8,128)(2,1)}, bf16[512,512]{1,0:T(8,128)(2,1)S(1)}, u32[]{:S(2)}, u32[]{:S(2)}) collective-permute-start(bf16[512,512]{1,0:T(8,128)(2,1)} %refs_0_.1), channel_id=1, source_target_pairs={{0,1},{1,0},{2,3},{3,2},{4,5},{5,4},{6,7},{7,6},{8,9},{9,8},{10,11... | collective-permute-start | bytes 1572872 | tf_op jit(solution)/shard_map/ppermute | solution.py:352
  1.2 16.7 %collective-permute-start.1 = (bf16[512,512]{1,0:T(8,128)(2,1)}, bf16[512,512]{1,0:T(8,128)(2,1)S(1)}, u32[]{:S(2)}, u32[]{:S(2)}) collective-permute-start(bf16[512,512]{1,0:T(8,128)(2,1)} %refs_0_.1), channel_id=1, source_target_pairs={{0,2},{1,3},{2,0},{3,1},{4,6},{5,7},{6,4},{7,5},{8,10},{9,11},{10,... | collective-permute-start | bytes 1572872 | tf_op jit(solution)/shard_map/ppermute | solution.py:352
  3.8 14.1 %collective-permute-start.2 = (bf16[64,512]{1,0:T(8,128)(2,1)}, bf16[64,512]{1,0:T(8,128)(2,1)S(1)}, u32[]{:S(2)}, u32[]{:S(2)}) collective-permute-start(bf16[64,512]{1,0:T(8,128)(2,1)} %bitcast.15), channel_id=1, source_target_pairs={{0,2},{1,3},{2,0},{3,1},{4,6},{5,7},{6,4},{7,5},{8,10},{9,11},{10,... | collective-permute-start | bytes 196616 | tf_op jit(solution)/shard_map/ppermute | solution.py:352
  3.9 7.9 %copy-start.1 = (bf16[512,32,128]{2,1,0:T(8,128)(2,1)S(1)}, bf16[512,32,128]{2,1,0:T(8,128)(2,1)}, u32[]{:S(2)}) copy-start(bf16[512,32,128]{2,1,0:T(8,128)(2,1)} %param.9) | copy-start | bytes 12582916
  11.7 6.3 %copy-start.8 = (bf16[512,64]{0,1:T(8,128)(2,1)S(1)}, bf16[512,64]{0,1:T(8,128)(2,1)}, u32[]{:S(2)}) copy-start(bf16[512,64]{0,1:T(8,128)(2,1)} %param.7) | copy-start | bytes 196612
  17.9 3.1 %copy-start.9 = (bf16[64,512]{1,0:T(8,128)(2,1)}, bf16[64,512]{1,0:T(8,128)(2,1)S(1)}, u32[]{:S(2)}) copy-start(bf16[64,512]{1,0:T(8,128)(2,1)S(1)} %collective-permute-done.2.refs_6_) | copy-start | bytes 196612
  17.9 2.1 copy-start.6
  17.9 2.2 collective-permute-start.3
  18.0 2.0 collective-permute-start.4
  18.5 1.6 collective-permute-start.5
  20.0 1.0 copy-start.10
  20.0 1.0 copy-start.5
  20.1 0.9 copy-start.11
  20.1 0.9 copy-start.7
  183.4 22.1 %copy-start.4 = (f32[576,512]{1,0:T(8,128)S(1)}, f32[576,512]{1,0:T(8,128)}, u32[]{:S(2)}) copy-start(f32[576,512]{1,0:T(8,128)} %get-tuple-element.35) | copy-start | bytes 3538948
  183.4 3.1 %collective-permute-start.8 = (f32[576,512]{1,0:T(8,128)}, f32[576,512]{1,0:T(8,128)S(1)}, u32[]{:S(2)}, u32[]{:S(2)}) collective-permute-start(f32[576,512]{1,0:T(8,128)} %get-tuple-element.38), channel_id=1, source_target_pairs={{0,1},{1,0},{2,3},{3,2},{4,5},{5,4},{6,7},{7,6},{8,9},{9,8},{10,11... | collective-permute-start | bytes 3538952 | tf_op jit(solution)/shard_map/ppermute | solution.py:352
  183.8 100.9 %collective-permute-start.18 = (f32[24,512,128]{2,1,0:T(8,128)}, f32[24,512,128]{2,1,0:T(8,128)}, u32[]{:S(2)}, u32[]{:S(2)}) collective-permute-start(f32[24,512,128]{2,1,0:T(8,128)} %get-tuple-element.43.mine), channel_id=1, source_target_pairs={{0,1},{1,0},{2,3},{3,2},{4,5},{5,4},{6,7},{7,6},{8,9},{9,8},{10,11... | collective-permute-start | bytes 18874376 | tf_op jit(solution)/shard_map/ppermute | solution.py:352
  184.0 13.4 %collective-permute-start.7 = (f32[576,512]{1,0:T(8,128)}, f32[576,512]{1,0:T(8,128)}, u32[]{:S(2)}, u32[]{:S(2)}) collective-permute-start(f32[576,512]{1,0:T(8,128)} %get-tuple-element.36), channel_id=1, source_target_pairs={{0,1},{1,0},{2,3},{3,2},{4,5},{5,4},{6,7},{7,6},{8,9},{9,8},{10,11... | collective-permute-start | bytes 3538952 | tf_op jit(solution)/shard_map/ppermute | solution.py:352
  188.9 19.6 %copy-start.2 = (f32[8,512,128]{2,1,0:T(8,128)S(1)}, f32[8,512,128]{2,1,0:T(8,128)}, u32[]{:S(2)}) copy-start(f32[8,512,128]{2,1,0:T(8,128)} %get-tuple-element.34) | copy-start | bytes 6291460
  188.9 16.5 %collective-permute-start.9 = (f32[576,256]{1,0:T(8,128)}, f32[576,256]{1,0:T(8,128)}, u32[]{:S(2)}, u32[]{:S(2)}) collective-permute-start(f32[576,256]{1,0:T(8,128)} %get-tuple-element.49), channel_id=1, source_target_pairs={{0,2},{1,3},{2,0},{3,1},{4,6},{5,7},{6,4},{7,5},{8,10},{9,11},{10,... | collective-permute-start | bytes 1769480 | tf_op jit(solution)/shard_map/ppermute | solution.py:352
  188.9 29.0 %collective-permute-start.11 = (f32[576,256]{1,0:T(8,128)}, f32[576,256]{1,0:T(8,128)S(1)}, u32[]{:S(2)}, u32[]{:S(2)}) collective-permute-start(f32[576,256]{1,0:T(8,128)} %get-tuple-element.48), channel_id=1, source_target_pairs={{0,2},{1,3},{2,0},{3,1},{4,6},{5,7},{6,4},{7,5},{8,10},{9,11},{10,... | collective-permute-start | bytes 1769480 | tf_op jit(solution)/shard_map/ppermute | solution.py:352
  206.9 7.9 %collective-permute-start.10 = (f32[288,256]{1,0:T(8,128)S(1)}, f32[288,256]{1,0:T(8,128)S(1)}, u32[]{:S(2)}, u32[]{:S(2)}) collective-permute-start(f32[288,256]{1,0:T(8,128)S(1)} %slice_select_fusion.1), channel_id=1, source_target_pairs={{0,4},{4,0},{8,12},{12,8},{1,5},{5,1},{9,13},{13,9},{2,6},{6,2},{1... | collective-permute-start | bytes 884744 | tf_op jit(solution)/shard_map/ppermute | solution.py:352
  208.5 53.8 %collective-permute-start.6 = (f32[8,512,128]{2,1,0:T(8,128)S(1)}, f32[8,512,128]{2,1,0:T(8,128)S(1)}, u32[]{:S(2)}, u32[]{:S(2)}) collective-permute-start(f32[8,512,128]{2,1,0:T(8,128)S(1)} %copy-done.2), channel_id=1, source_target_pairs={{0,2},{1,3},{2,0},{3,1},{4,6},{5,7},{6,4},{7,5},{8,10},{9,11},{10,... | collective-permute-start | bytes 6291464 | tf_op jit(solution)/shard_map/ppermute | solution.py:352
  219.2 14.1 %collective-permute-start.14 = (f32[288,256]{1,0:T(8,128)S(1)}, f32[288,256]{1,0:T(8,128)S(1)}, u32[]{:S(2)}, u32[]{:S(2)}) collective-permute-start(f32[288,256]{1,0:T(8,128)S(1)} %slice_select_fusion), channel_id=1, source_target_pairs={{0,4},{4,0},{8,12},{12,8},{1,5},{5,1},{9,13},{13,9},{2,6},{6,2},{1... | collective-permute-start | bytes 884744 | tf_op jit(solution)/shard_map/ppermute | solution.py:352
  220.9 19.6 %collective-permute-start.12 = (f32[288,256]{1,0:T(8,128)S(1)}, f32[288,256]{1,0:T(8,128)S(1)}, u32[]{:S(2)}, u32[]{:S(2)}) collective-permute-start(f32[288,256]{1,0:T(8,128)S(1)} %select_add_fusion.1), channel_id=1, source_target_pairs={{0,8},{4,12},{8,0},{12,4},{1,9},{5,13},{9,1},{13,5},{2,10},{6,14},... | collective-permute-start | bytes 884744 | tf_op jit(solution)/shard_map/ppermute | solution.py:352
  233.4 15.0 %collective-permute-start.15 = (f32[288,256]{1,0:T(8,128)S(1)}, f32[288,256]{1,0:T(8,128)S(1)}, u32[]{:S(2)}, u32[]{:S(2)}) collective-permute-start(f32[288,256]{1,0:T(8,128)S(1)} %select_add_fusion), channel_id=1, source_target_pairs={{0,8},{4,12},{8,0},{12,4},{1,9},{5,13},{9,1},{13,5},{2,10},{6,14},... | collective-permute-start | bytes 884744 | tf_op jit(solution)/shard_map/ppermute | solution.py:352
  240.5 11.4 %collective-permute-start.13 = (f32[288,256]{1,0:T(8,128)S(1)}, f32[288,256]{1,0:T(8,128)S(1)}, u32[]{:S(2)}, u32[]{:S(2)}) collective-permute-start(f32[288,256]{1,0:T(8,128)S(1)} %add.38), channel_id=1, source_target_pairs={{0,4},{4,0},{8,12},{12,8},{1,5},{5,1},{9,13},{13,9},{2,6},{6,2},{1... | collective-permute-start | bytes 884744 | tf_op jit(solution)/shard_map/ppermute | solution.py:352
  248.5 13.9 %copy-start.3 = (f32[8,512,128]{2,1,0:T(8,128)S(1)}, f32[8,512,128]{2,1,0:T(8,128)}, u32[]{:S(2)}) copy-start(f32[8,512,128]{2,1,0:T(8,128)} %get-tuple-element.34) | copy-start | bytes 6291460
  248.5 9.3 %collective-permute-start.16 = (f32[288,256]{1,0:T(8,128)S(1)}, f32[288,256]{1,0:T(8,128)S(1)}, u32[]{:S(2)}, u32[]{:S(2)}) collective-permute-start(f32[288,256]{1,0:T(8,128)S(1)} %add.42), channel_id=1, source_target_pairs={{0,4},{4,0},{8,12},{12,8},{1,5},{5,1},{9,13},{13,9},{2,6},{6,2},{1... | collective-permute-start | bytes 884744 | tf_op jit(solution)/shard_map/ppermute | solution.py:352
  262.6 8.6 %copy-start = (f32[8,512,128]{2,1,0:T(8,128)}, f32[8,512,128]{2,1,0:T(8,128)S(1)}, u32[]{:S(2)}) copy-start(f32[8,512,128]{2,1,0:T(8,128)S(1)} %add.43.mine) | copy-start | bytes 6291460
  262.6 37.0 %collective-permute-start.17 = (f32[8,512,128]{2,1,0:T(8,128)S(1)}, f32[8,512,128]{2,1,0:T(8,128)}, u32[]{:S(2)}, u32[]{:S(2)}) collective-permute-start(f32[8,512,128]{2,1,0:T(8,128)S(1)} %add.43.mine), channel_id=1, source_target_pairs={{0,1},{1,0},{2,3},{3,2},{4,5},{5,4},{6,7},{7,6},{8,9},{9,8},{10,11... | collective-permute-start | bytes 6291464 | tf_op jit(solution)/shard_map/ppermute | solution.py:352

commit v3 on v2

--- a/solution.py
+++ b/solution.py
@@ -10,7 +10,7 @@
 LOG2E = 1.4426950408889634
 F32 = jnp.float32
 BF16 = jnp.bfloat16
-Y_HEADS = 24
+Y_HEADS = 25
 
 
 def mm(a, b):
@@ -63,6 +63,7 @@
         to_mate(g, slot).wait()
         chip[g] += own[slot]
 
+    def pass_on(g):
         @pl.when(g < n_y)
         def _():
             to_across(g).start()
@@ -219,6 +220,10 @@
         def _():
             to_mate(h - 1, lax.rem(h + 1, 2)).start()
 
+        @pl.when(h >= 2)
+        def _():
+            pass_on(h - 2)
+
     @pl.when(h == n_h)
     def _():
         w_old = jnp.concatenate([wk_old[0], wv_old[0]], axis=1)
@@ -227,9 +232,11 @@
         for j in range(n_blk):
             acc_refs[j][blk:, :] = dr_s[j * blk:(j + 1) * blk, :].T[:d_rope, :]
         post_out()
+        merge(n_h - 2, n_h % 2)
         to_mate(n_h - 1, (n_h - 1) % 2).start()
-        merge(n_h - 2, n_h % 2)
+        pass_on(n_h - 2)
         merge(n_h - 1, (n_h - 1) % 2)
+        pass_on(n_h - 1)
 
         def finish(g, carry):
             to_across(g).wait()
@@ -296,33 +303,38 @@
     )(*args)
 
 
-def place_body(mine, other, *refs):
+def place_body(n_in, *refs):
+    mine, other = refs[:n_in], refs[n_in:2 * n_in]
     k_ref, v_ref = refs[-2:]
     even = lax.rem(lax.axis_index('cp'), 2) == 0
-    for j in range(mine.shape[0]):
-        a, b = mine[j], other[j]
-        k_ref[:, j, :] = jnp.where(even, a, b)
-        v_ref[:, j, :] = jnp.where(even, b, a)
-
-
-def place(group, heads, mine, other, carry):
+    o = 0
+    for x, y in zip(mine, other):
+        for j in range(x.shape[0]):
+            a, b = x[j], y[j]
+            k_ref[:, o, :] = jnp.where(even, a, b)
+            v_ref[:, o, :] = jnp.where(even, b, a)
+            o += 1
+
+
+def place(group, n_group, heads, parts, carry):
     n_g = 8
-    n_h, rank, d_val = mine.shape
+    _, rank, d_val = parts[0][0].shape
     step = 128
-    ins = [pl.BlockSpec((n_g, step, d_val), lambda g, r: (g, r, 0))] * 2
-    args = [mine, other]
+    ins = [pl.BlockSpec((size, step, d_val), lambda g, r, first=first: (g + first, r, 0)) for _, _, size, first in parts] * 2
+    args = [p[0] for p in parts] + [p[1] for p in parts]
+    n = len(args)
     aliases = {}
     if carry is not None:
-        aliases = {2: 0, 3: 1}
+        aliases = {n: 0, n + 1: 1}
         args += list(carry)
         ins = ins + [pl.BlockSpec(memory_space=pl.ANY)] * 2
     out = jax.ShapeDtypeStruct((rank, heads, d_val), F32)
     return pl.pallas_call(
-        place_body, grid=(n_h // n_g, rank // step), in_specs=ins,
+        functools.partial(place_body, len(parts)), grid=(n_group, rank // step), in_specs=ins,
         out_specs=[pl.BlockSpec((step, n_g, d_val), lambda g, r: (r, g + group, 0))] * 2,
         out_shape=[out, out], input_output_aliases=aliases,
         compiler_params=pltpu.CompilerParams(dimension_semantics=("arbitrary", "arbitrary")),
-        cost_estimate=pl.CostEstimate(flops=n_h * 10 ** 8, bytes_accessed=4 * n_h * rank * d_val * 4, transcendentals=0),
+        cost_estimate=pl.CostEstimate(flops=n_group * 10 ** 9, bytes_accessed=4 * n_group * 8 * rank * d_val * 4, transcendentals=0),
         name="place",
     )(*args)
 
@@ -380,7 +392,9 @@
         dq = jnp.transpose(dqt * scale, (2, 0, 1))
         out = to_rows(ot)
         other = swap(done, 'cp', n_cp, 1)
-        placed = place(0, heads, done, other, None)
+        whole = Y_HEADS // 8
+        placed = place(0, 1, heads, [(done, other, 8, 0)], None)
+        placed = place(1, whole - 1, heads, [(done, other, 8, 1)], placed)
         odd = lax.rem(lax.axis_index('tp'), 2) == 1
         n_col = a0.shape[1] // 2
         mid = a0.shape[0] // 2
@@ -408,7 +422,9 @@
         far = swap(part, 'cp', n_cp, 2)
         far, acc = lax.optimization_barrier((far, acc))
         total = part + far
-        placed = place(Y_HEADS // 8, heads, total, swap(total, 'cp', n_cp, 1), placed)
+        rest = Y_HEADS - whole * 8
+        placed = place(whole, 1, heads, [(done, other, rest, Y_HEADS // rest - 1),
+                                         (total, swap(total, 'cp', n_cp, 1), heads - Y_HEADS, 0)], placed)
         return (out, dq, acc[:rows], acc[rows:].T, placed[0], placed[1])
 
     return jax.shard_map(device_body, mesh=mesh,

time: 306 us -> 305 us (level)
  waiting for transfers between devices: 66.5 us -> 60.7 us
  Pallas kernels: 191 us -> 195 us
    ppermute x19, waiting for transfers between devices: 66.5 us -> 60.7 us  [swap(): return lax.ppermute(x, axis, [(i, i ^ bit) for i in range(size)])]
    pallas_call x2 -> x3, Pallas kernels: 20.5 us -> 21.5 us  [place(): pl.pallas_call(functools.partial(place_body, len(parts)), grid=(n_group,...]
  transfers between devices with their start and end apart: 19 -> 19, of which waited for: 14 -> 13; matrix products, arithmetic and copies ran while one was open for 10% -> 10% of each run, Pallas kernels for 8% -> 8%
where the time goes in v3:
time: 305 us; the launch traced here: 304 us
  Pallas kernels  195 us (64%)
  waiting for transfers between devices  60.7 us (20%)
  other arithmetic  17.7 us (6%)
  starting transfers between devices  15.7 us (5%)
  local copies, waits for them, and re-layouts  14.1 us (5%)
    pallas_call x1, Pallas kernels, attn_call(): pl.pallas_call(functools.partial(attn_body, n_cp, half, scale, n_h, n_y),...  165 us
    ppermute x19, waiting for transfers between devices, swap(): return lax.ppermute(x, axis, [(i, i ^ bit) for i in range(size)])  60.7 us
    pallas_call x3, Pallas kernels, place(): pl.pallas_call(functools.partial(place_body, len(parts)), grid=(n_group,...  21.5 us
    ppermute x19, starting transfers between devices, swap(): return lax.ppermute(x, axis, [(i, i ^ bit) for i in range(size)])  15.7 us
    transpose x1, other arithmetic, device_body(): dq = jnp.transpose(dqt * scale, (2, 0, 1))  11.8 us
    pallas_call x1, Pallas kernels, to_rows(): pl.pallas_call(rows_body, grid=(heads // n_g,), in_specs=[pl.BlockSpec((n...  8.45 us
    transpose x1, local copies, waits for them, and re-layouts, device_body(): wv_h = jnp.transpose(w_uv, (1, 0, 2))  7.85 us
  transfers between devices with their start and end apart: 19, of which 13 were waited for; matrix products, arithmetic and copies ran while one was open for 10% of the time, Pallas kernels for 8%

profile of v3, /device:TPU:0, one launch (start us, length us, event | category | flops | bytes accessed | tf_op | source)
XLA Modules:
  0.0 303.8 jit_solution(2632257221253763936)
XLA Ops:
  0.6 0.6 collective-permute-start
  1.2 2.6 collective-permute-start.1
  3.8 0.1 collective-permute-start.2
  3.9 7.9 %copy_bitcast_fusion = (bf16[32,512,128]{2,1,0:T(8,128)(2,1)}, bf16[32,512,128]{2,1,0:T(8,128)(2,1)}) fusion(bf16[512,32,128]{2,1,0:T(8,128)(2,1)} %param.11, bf16[512,32,128]{2,1,0:T(8,128)(2,1)} %param.10), kind=kLoop, calls=%fused_computation.1 | loop fusion | bytes 16777216 | tf_op jit(solution)/shard_map/transpose | solution.py:385
  11.7 3.6 %copy.22 = bf16[512,32,128]{2,0,1:T(8,128)(2,1)} copy(bf16[512,32,128]{2,1,0:T(8,128)(2,1)S(1)} %copy-done.1) | data formatting | bytes 8388608 | tf_op args[3]
  15.4 2.5 collective-permute-done.2.refs_6_
  17.9 0.1 collective-permute-start.3
  18.0 0.5 collective-permute-start.4
  18.5 0.1 collective-permute-start.5
  18.6 1.4 collective-permute-done.4.refs_5_
  20.0 0.1 collective-permute-done.5.refs_7_
  20.1 0.9 copy-done.7
  21.0 164.8 %attn.1 = (bf16[32,128,512]{2,1,0:T(8,128)(2,1)}, f32[32,192,512]{2,1,0:T(8,128)}, f32[576,512]{1,0:T(8,128)}, f32[576,512]{1,0:T(8,128)}, f32[576,512]{1,0:T(8,...) custom-call(bf16[512,512]{1,0:T(8,128)(2,1)} %refs_0_.1, bf16[512,512]{1,0:T(8,128)(2,1)} %copy-done.5, ...), custom_call_target="tpu_custom_call" | custom-call | flops 90194313216 | bytes 33554432 | tf_op jit(solution)/shard_map/attn/pallas_call | solution.py:295
  185.8 0.1 collective-permute-start.8
  185.9 0.5 collective-permute-start.17
  186.4 0.1 collective-permute-start.7
  186.4 2.5 collective-permute-done.8
  188.9 2.4 slice_add_fusion.1
  191.3 1.4 collective-permute-start.9
  192.7 0.6 collective-permute-start.11
  193.3 6.8 %collective-permute-done.7 = f32[576,512]{1,0:T(8,128)} collective-permute-done((f32[576,512]{1,0:T(8,128)}, f32[576,512]{1,0:T(8,128)}, u32[]{:S(2)}, u32[]{:S(2)}) %collective-permute-start.7) | collective-permute-done | bytes 1179680 | tf_op jit(solution)/shard_map/ppermute | solution.py:364
  200.1 7.7 %collective-permute-done.9 = f32[576,256]{1,0:T(8,128)} collective-permute-done((f32[576,256]{1,0:T(8,128)}, f32[576,256]{1,0:T(8,128)}, u32[]{:S(2)}, u32[]{:S(2)}) %collective-permute-start.9) | collective-permute-done | bytes 589856 | tf_op jit(solution)/shard_map/ppermute | solution.py:364
  207.8 1.5 fusion.1
  209.4 1.6 collective-permute-start.10
  211.1 1.4 collective-permute-start.6
  212.4 4.4 %collective-permute-done.10 = f32[288,256]{1,0:T(8,128)S(1)} collective-permute-done((f32[288,256]{1,0:T(8,128)S(1)}, f32[288,256]{1,0:T(8,128)S(1)}, u32[]{:S(2)}, u32[]{:S(2)}) %collective-permute-start.10) | collective-permute-done | bytes 294944 | tf_op jit(solution)/shard_map/ppermute | solution.py:364
  216.9 3.5 %collective-permute-done.11 = f32[576,256]{1,0:T(8,128)S(1)} collective-permute-done((f32[576,256]{1,0:T(8,128)}, f32[576,256]{1,0:T(8,128)S(1)}, u32[]{:S(2)}, u32[]{:S(2)}) %collective-permute-start.11) | collective-permute-done | bytes 589856 | tf_op jit(solution)/shard_map/ppermute | solution.py:364
  220.4 1.2 fusion
  221.6 1.6 collective-permute-start.14
  223.3 2.6 collective-permute-start.12
  225.9 9.4 %collective-permute-done.14 = f32[288,256]{1,0:T(8,128)S(1)} collective-permute-done((f32[288,256]{1,0:T(8,128)S(1)}, f32[288,256]{1,0:T(8,128)S(1)}, u32[]{:S(2)}, u32[]{:S(2)}) %collective-permute-start.14) | collective-permute-done | bytes 294944 | tf_op jit(solution)/shard_map/ppermute | solution.py:364
  235.3 0.6 collective-permute-start.15
  236.0 6.4 %collective-permute-done.12 = f32[288,256]{1,0:T(8,128)S(1)} collective-permute-done((f32[288,256]{1,0:T(8,128)S(1)}, f32[288,256]{1,0:T(8,128)S(1)}, u32[]{:S(2)}, u32[]{:S(2)}) %collective-permute-start.12) | collective-permute-done | bytes 294944 | tf_op jit(solution)/shard_map/ppermute | solution.py:364
  242.4 1.1 collective-permute-start.13
  243.6 6.8 %collective-permute-done.15 = f32[288,256]{1,0:T(8,128)S(1)} collective-permute-done((f32[288,256]{1,0:T(8,128)S(1)}, f32[288,256]{1,0:T(8,128)S(1)}, u32[]{:S(2)}, u32[]{:S(2)}) %collective-permute-start.15) | collective-permute-done | bytes 294944 | tf_op jit(solution)/shard_map/ppermute | solution.py:364
  250.4 0.1 collective-permute-start.16
  250.5 3.4 %collective-permute-done.13 = f32[288,256]{1,0:T(8,128)S(1)} collective-permute-done((f32[288,256]{1,0:T(8,128)S(1)}, f32[288,256]{1,0:T(8,128)S(1)}, u32[]{:S(2)}, u32[]{:S(2)}) %collective-permute-start.13) | collective-permute-done | bytes 294944 | tf_op jit(solution)/shard_map/ppermute | solution.py:364
  253.9 5.9 %collective-permute-done.16 = f32[288,256]{1,0:T(8,128)S(1)} collective-permute-done((f32[288,256]{1,0:T(8,128)S(1)}, f32[288,256]{1,0:T(8,128)S(1)}, u32[]{:S(2)}, u32[]{:S(2)}) %collective-permute-start.16) | collective-permute-done | bytes 294944 | tf_op jit(solution)/shard_map/ppermute | solution.py:364
  259.8 0.1 maximum_maximum_fusion
  259.9 0.2 add.43.refs_1_
  260.2 0.1 collective-permute-start.18
  260.2 8.5 %to_rows.1 = bf16[512,32,128]{2,1,0:T(8,128)(2,1)} custom-call(bf16[32,128,512]{2,1,0:T(8,128)(2,1)} %get-tuple-element.34.x_ref), custom_call_target="tpu_custom_call" | custom-call | flops 1000000000 | bytes 8388608 | tf_op jit(solution)/shard_map/to_rows/pallas_call | solution.py:351
  268.7 11.8 %multiply_bitcast_fusion = f32[512,32,192]{0,2,1:T(8,128)} fusion(f32[32,192,512]{2,1,0:T(8,128)} %get-tuple-element.35), kind=kLoop, calls=%fused_computation | loop fusion | flops 3145728 | bytes 25165824 | tf_op jit(solution)/shard_map/transpose | solution.py:392
  280.5 1.0 slice.54
  281.6 0.7 slice_bitcast_fusion
  282.2 5.7 %place.3 = (f32[512,32,128]{2,1,0:T(8,128)}, f32[512,32,128]{2,1,0:T(8,128)}) custom-call(f32[25,512,128]{2,1,0:T(8,128)} %get-tuple-element.44.refs_0_, f32[25,512,128]{2,1,0:T(8,128)} %collective-permute-done.17.refs_1_.refs_2_), custom_call_target="tpu_custom_call" | custom-call | flops 1000000000 | bytes 8388608 | tf_op jit(solution)/shard_map/place/pallas_call | solution.py:332
  287.9 10.2 %place.4 = (f32[512,32,128]{2,1,0:T(8,128)}, f32[512,32,128]{2,1,0:T(8,128)}) custom-call(f32[25,512,128]{2,1,0:T(8,128)} %get-tuple-element.44.refs_0_, f32[25,512,128]{2,1,0:T(8,128)} %collective-permute-done.17.refs_1_.refs_2_, f32[512,32,128]{2,1,0:T(8,128)} %get-tuple-element.46.refs_2_, ...), custom_call_target="tpu_custom_call", output_to_operand_aliasing={{0}: (2, {}), {1}: (3, {})} | custom-call | flops 2000000000 | bytes 16777216 | tf_op jit(solution)/shard_map/place/pallas_call | solution.py:332
  298.1 5.7 %place.5 = (f32[512,32,128]{2,1,0:T(8,128)}, f32[512,32,128]{2,1,0:T(8,128)}) custom-call(f32[25,512,128]{2,1,0:T(8,128)} %get-tuple-element.44.refs_0_, f32[7,512,128]{2,1,0:T(8,128)} %copy-done, f32[25,512,128]{2,1,0:T(8,128)} %collective-permute-done.17.refs_1_.refs_2_, ...), custom_call_target="tpu_custom_call", output_to_operand_aliasing={{0}: (4, {}), {1}: (5, {})} | custom-call | flops 1000000000 | bytes 8388608 | tf_op jit(solution)/shard_map/place/pallas_call | solution.py:332
  (37 shorter events, 0.4 us)
Async XLA Ops:
  0.6 19.3 %collective-permute-start = (bf16[512,512]{1,0:T(8,128)(2,1)}, bf16[512,512]{1,0:T(8,128)(2,1)S(1)}, u32[]{:S(2)}, u32[]{:S(2)}) collective-permute-start(bf16[512,512]{1,0:T(8,128)(2,1)} %refs_0_.1), channel_id=1, source_target_pairs={{0,1},{1,0},{2,3},{3,2},{4,5},{5,4},{6,7},{7,6},{8,9},{9,8},{10,11... | collective-permute-start | bytes 1572872 | tf_op jit(solution)/shard_map/ppermute | solution.py:364
  1.2 16.7 %collective-permute-start.1 = (bf16[512,512]{1,0:T(8,128)(2,1)}, bf16[512,512]{1,0:T(8,128)(2,1)S(1)}, u32[]{:S(2)}, u32[]{:S(2)}) collective-permute-start(bf16[512,512]{1,0:T(8,128)(2,1)} %refs_0_.1), channel_id=1, source_target_pairs={{0,2},{1,3},{2,0},{3,1},{4,6},{5,7},{6,4},{7,5},{8,10},{9,11},{10,... | collective-permute-start | bytes 1572872 | tf_op jit(solution)/shard_map/ppermute | solution.py:364
  3.8 7.9 %copy-start.1 = (bf16[512,32,128]{2,1,0:T(8,128)(2,1)S(1)}, bf16[512,32,128]{2,1,0:T(8,128)(2,1)}, u32[]{:S(2)}) copy-start(bf16[512,32,128]{2,1,0:T(8,128)(2,1)} %param.9) | copy-start | bytes 12582916
  3.8 14.1 %collective-permute-start.2 = (bf16[64,512]{1,0:T(8,128)(2,1)}, bf16[64,512]{1,0:T(8,128)(2,1)S(1)}, u32[]{:S(2)}, u32[]{:S(2)}) collective-permute-start(bf16[64,512]{1,0:T(8,128)(2,1)} %bitcast.15), channel_id=1, source_target_pairs={{0,2},{1,3},{2,0},{3,1},{4,6},{5,7},{6,4},{7,5},{8,10},{9,11},{10,... | collective-permute-start | bytes 196616 | tf_op jit(solution)/shard_map/ppermute | solution.py:364
  11.7 6.3 %copy-start.8 = (bf16[512,64]{0,1:T(8,128)(2,1)S(1)}, bf16[512,64]{0,1:T(8,128)(2,1)}, u32[]{:S(2)}) copy-start(bf16[512,64]{0,1:T(8,128)(2,1)} %param.7) | copy-start | bytes 196612
  17.9 3.1 %copy-start.9 = (bf16[64,512]{1,0:T(8,128)(2,1)}, bf16[64,512]{1,0:T(8,128)(2,1)S(1)}, u32[]{:S(2)}) copy-start(bf16[64,512]{1,0:T(8,128)(2,1)S(1)} %collective-permute-done.2.refs_6_) | copy-start | bytes 196612
  17.9 2.1 copy-start.6
  17.9 2.2 collective-permute-start.3
  18.0 2.0 collective-permute-start.4
  18.5 1.6 collective-permute-start.5
  20.0 1.0 copy-start.10
  20.0 1.0 copy-start.5
  20.1 0.9 copy-start.11
  20.1 0.9 copy-start.7
  185.8 25.3 %copy-start.2 = (f32[7,512,128]{2,1,0:T(8,128)S(1)}, f32[7,512,128]{2,1,0:T(8,128)}, u32[]{:S(2)}) copy-start(f32[7,512,128]{2,1,0:T(8,128)} %get-tuple-element.36) | copy-start | bytes 5505028
  185.8 34.6 %copy-start.4 = (f32[576,512]{1,0:T(8,128)S(1)}, f32[576,512]{1,0:T(8,128)}, u32[]{:S(2)}) copy-start(f32[576,512]{1,0:T(8,128)} %get-tuple-element.37) | copy-start | bytes 3538948
  185.8 3.1 %collective-permute-start.8 = (f32[576,512]{1,0:T(8,128)}, f32[576,512]{1,0:T(8,128)S(1)}, u32[]{:S(2)}, u32[]{:S(2)}) collective-permute-start(f32[576,512]{1,0:T(8,128)} %get-tuple-element.40), channel_id=1, source_target_pairs={{0,1},{1,0},{2,3},{3,2},{4,5},{5,4},{6,7},{7,6},{8,9},{9,8},{10,11... | collective-permute-start | bytes 3538952 | tf_op jit(solution)/shard_map/ppermute | solution.py:364
  185.9 96.4 %collective-permute-start.17 = (f32[25,512,128]{2,1,0:T(8,128)}, f32[25,512,128]{2,1,0:T(8,128)}, u32[]{:S(2)}, u32[]{:S(2)}) collective-permute-start(f32[25,512,128]{2,1,0:T(8,128)} %get-tuple-element.44.refs_0_), channel_id=1, source_target_pairs={{0,1},{1,0},{2,3},{3,2},{4,5},{5,4},{6,7},{7,6},{8,9},{9,8},{10,11... | collective-permute-start | bytes 19660808 | tf_op jit(solution)/shard_map/ppermute | solution.py:364
  186.4 13.7 %collective-permute-start.7 = (f32[576,512]{1,0:T(8,128)}, f32[576,512]{1,0:T(8,128)}, u32[]{:S(2)}, u32[]{:S(2)}) collective-permute-start(f32[576,512]{1,0:T(8,128)} %get-tuple-element.38), channel_id=1, source_target_pairs={{0,1},{1,0},{2,3},{3,2},{4,5},{5,4},{6,7},{7,6},{8,9},{9,8},{10,11... | collective-permute-start | bytes 3538952 | tf_op jit(solution)/shard_map/ppermute | solution.py:364
  191.3 16.5 %collective-permute-start.9 = (f32[576,256]{1,0:T(8,128)}, f32[576,256]{1,0:T(8,128)}, u32[]{:S(2)}, u32[]{:S(2)}) collective-permute-start(f32[576,256]{1,0:T(8,128)} %get-tuple-element.53), channel_id=1, source_target_pairs={{0,2},{1,3},{2,0},{3,1},{4,6},{5,7},{6,4},{7,5},{8,10},{9,11},{10,... | collective-permute-start | bytes 1769480 | tf_op jit(solution)/shard_map/ppermute | solution.py:364
  192.7 27.7 %collective-permute-start.11 = (f32[576,256]{1,0:T(8,128)}, f32[576,256]{1,0:T(8,128)S(1)}, u32[]{:S(2)}, u32[]{:S(2)}) collective-permute-start(f32[576,256]{1,0:T(8,128)} %get-tuple-element.52), channel_id=1, source_target_pairs={{0,2},{1,3},{2,0},{3,1},{4,6},{5,7},{6,4},{7,5},{8,10},{9,11},{10,... | collective-permute-start | bytes 1769480 | tf_op jit(solution)/shard_map/ppermute | solution.py:364
  209.4 7.4 %collective-permute-start.10 = (f32[288,256]{1,0:T(8,128)S(1)}, f32[288,256]{1,0:T(8,128)S(1)}, u32[]{:S(2)}, u32[]{:S(2)}) collective-permute-start(f32[288,256]{1,0:T(8,128)S(1)} %slice_select_fusion.1), channel_id=1, source_target_pairs={{0,4},{4,0},{8,12},{12,8},{1,5},{5,1},{9,13},{13,9},{2,6},{6,2},{1... | collective-permute-start | bytes 884744 | tf_op jit(solution)/shard_map/ppermute | solution.py:364
  211.1 48.9 %collective-permute-start.6 = (f32[7,512,128]{2,1,0:T(8,128)S(1)}, f32[7,512,128]{2,1,0:T(8,128)S(1)}, u32[]{:S(2)}, u32[]{:S(2)}) collective-permute-start(f32[7,512,128]{2,1,0:T(8,128)S(1)} %copy-done.2), channel_id=1, source_target_pairs={{0,2},{1,3},{2,0},{3,1},{4,6},{5,7},{6,4},{7,5},{8,10},{9,11},{10,... | collective-permute-start | bytes 5505032 | tf_op jit(solution)/shard_map/ppermute | solution.py:364
  221.6 38.4 %copy-start.3 = (f32[7,512,128]{2,1,0:T(8,128)S(1)}, f32[7,512,128]{2,1,0:T(8,128)}, u32[]{:S(2)}) copy-start(f32[7,512,128]{2,1,0:T(8,128)} %get-tuple-element.36) | copy-start | bytes 5505028
  221.6 13.6 %collective-permute-start.14 = (f32[288,256]{1,0:T(8,128)S(1)}, f32[288,256]{1,0:T(8,128)S(1)}, u32[]{:S(2)}, u32[]{:S(2)}) collective-permute-start(f32[288,256]{1,0:T(8,128)S(1)} %slice_select_fusion), channel_id=1, source_target_pairs={{0,4},{4,0},{8,12},{12,8},{1,5},{5,1},{9,13},{13,9},{2,6},{6,2},{1... | collective-permute-start | bytes 884744 | tf_op jit(solution)/shard_map/ppermute | solution.py:364
  223.3 19.1 %collective-permute-start.12 = (f32[288,256]{1,0:T(8,128)S(1)}, f32[288,256]{1,0:T(8,128)S(1)}, u32[]{:S(2)}, u32[]{:S(2)}) collective-permute-start(f32[288,256]{1,0:T(8,128)S(1)} %select_add_fusion.1), channel_id=1, source_target_pairs={{0,8},{4,12},{8,0},{12,4},{1,9},{5,13},{9,1},{13,5},{2,10},{6,14},... | collective-permute-start | bytes 884744 | tf_op jit(solution)/shard_map/ppermute | solution.py:364
  235.3 15.0 %collective-permute-start.15 = (f32[288,256]{1,0:T(8,128)S(1)}, f32[288,256]{1,0:T(8,128)S(1)}, u32[]{:S(2)}, u32[]{:S(2)}) collective-permute-start(f32[288,256]{1,0:T(8,128)S(1)} %select_add_fusion), channel_id=1, source_target_pairs={{0,8},{4,12},{8,0},{12,4},{1,9},{5,13},{9,1},{13,5},{2,10},{6,14},... | collective-permute-start | bytes 884744 | tf_op jit(solution)/shard_map/ppermute | solution.py:364
  242.4 11.4 %collective-permute-start.13 = (f32[288,256]{1,0:T(8,128)S(1)}, f32[288,256]{1,0:T(8,128)S(1)}, u32[]{:S(2)}, u32[]{:S(2)}) collective-permute-start(f32[288,256]{1,0:T(8,128)S(1)} %add.38), channel_id=1, source_target_pairs={{0,4},{4,0},{8,12},{12,8},{1,5},{5,1},{9,13},{13,9},{2,6},{6,2},{1... | collective-permute-start | bytes 884744 | tf_op jit(solution)/shard_map/ppermute | solution.py:364
  250.4 9.3 %collective-permute-start.16 = (f32[288,256]{1,0:T(8,128)S(1)}, f32[288,256]{1,0:T(8,128)S(1)}, u32[]{:S(2)}, u32[]{:S(2)}) collective-permute-start(f32[288,256]{1,0:T(8,128)S(1)} %add.42), channel_id=1, source_target_pairs={{0,4},{4,0},{8,12},{12,8},{1,5},{5,1},{9,13},{13,9},{2,6},{6,2},{1... | collective-permute-start | bytes 884744 | tf_op jit(solution)/shard_map/ppermute | solution.py:364
  260.1 8.5 %copy-start = (f32[7,512,128]{2,1,0:T(8,128)}, f32[7,512,128]{2,1,0:T(8,128)S(1)}, u32[]{:S(2)}) copy-start(f32[7,512,128]{2,1,0:T(8,128)S(1)} %add.43.refs_1_) | copy-start | bytes 5505028
  260.2 37.9 %collective-permute-start.18 = (f32[7,512,128]{2,1,0:T(8,128)S(1)}, f32[7,512,128]{2,1,0:T(8,128)}, u32[]{:S(2)}, u32[]{:S(2)}) collective-permute-start(f32[7,512,128]{2,1,0:T(8,128)S(1)} %add.43.refs_1_), channel_id=1, source_target_pairs={{0,1},{1,0},{2,3},{3,2},{4,5},{5,4},{6,7},{7,6},{8,9},{9,8},{10,11... | collective-permute-start | bytes 5505032 | tf_op jit(solution)/shard_map/ppermute | solution.py:364
